TPU v7x, 256 devices: a whole 4x4x8 slice. The times are simulated.
256 devices in a mesh: dev: 256 (over x, y, z, core).
Axes of the slice: x: 4, y: 4, z: 8, core: 2. Of those that a mesh axis runs over, the one named last changes fastest.
Arguments:
- field: float32 [16, 16, 16, 32768], P(None, None, None, 'dev'), may hold values from -6 to 6
- s_mats: float32 [3, 18, 18], replicated, may hold values from -1.5 to 1.5
- lam: float32 [3, 18], replicated, may hold values from 0.2 to 4
- coeff: float32 [3, 32768], P(None, 'dev'), may hold values from 0.5 to 2
- nbr_src: int32 [6, 32768], P(None, 'dev'), may hold values from 0 to 7, as said below
- nbr_idx: int32 [6, 32768], P(None, 'dev'), may hold values from 0 to 767, as said below
- orient: int32 [6, 32768], P(None, 'dev'), may hold values from 0 to 3, as said below
- send_x: int32 [2, 4096], P(None, 'dev'), may hold values from 0 to 255, as said below
- send_y: int32 [2, 4096], P(None, 'dev'), may hold values from 256 to 511, as said below
- send_z: int32 [2, 16384], P(None, 'dev'), may hold values from 512 to 767, as said below
Outputs:
- smoothed: float32 [16, 16, 16, 32768], P(None, None, None, 'dev')
Inputs may be any that keep to these rules, and one draw needn't show every extreme that they name: `nbr_src`: 0 where the face lies on the boundary of the box of elements, 1 where the element across it is on the same device, 2 + j where it is on the device whose index is lower by o_j. Devices form a 4 x 4 x 16 grid, first index fastest; each holds a 8 x 8 x 2 block of the box, its elements in slots in any order and each stored mirrored or not along each of its three axes. Every face not on the boundary is shared by exactly two elements and listed from both sides. `nbr_idx`: for code 1 the id g * 128 + s of the face g of the element in slot s that meets this face; for code 2 + j a position in list j of the sending device; 0 for code 0. `orient`: the two sides of a shared face carry the same code; 0 on the boundary. `send_x`: row r (list r) holds the ids of the 16 faces of this device's block on its low (r = 0) or high (r = 1) side across the first dimension, each once, ordered by the faces' block coordinates along the second dimension, then the third; the device whose index is higher by o_r reads it. Each id is that of face 0 or 1 of its element. `send_y`: as send_x, across the second dimension (lists 2 and 3), 16 faces ordered by the first block coordinate, then the third; each id is that of face 2 or 3 of its element. `send_z`: as send_x, across the third dimension (lists 4 and 5), 64 faces ordered by the first block coordinate, then the second; each id is that of face 4 or 5 of its element.
All inputs are finite; a program needn't handle non-finite values.
Results may differ from a plain program's by a relative error of at most 0.0003.
Values sent between devices are 32-bit elements; how exact they have to be, the bound alone decides.
A program may use at most 128 MiB of HBM per device.

v0:
```python
import functools

import jax
import jax.numpy as jnp
import numpy as np
from jax import lax
from jax.experimental import pallas as pl
from jax.experimental.pallas import tpu as pltpu
from jax.sharding import PartitionSpec as P

NP = 16
NE = 18
SLOTS = 128
ROWS = 336
RIM = 320
COUNTS = (16, 16, 64)
STARTS = (0, 32, 64)
OFFSETS = (-1, 1, -4, 4, -16, 16)
BF = jnp.bfloat16
F32 = jnp.float32
VMEM = pl.BlockSpec(memory_space=pltpu.VMEM)


def make_tables():
    r = np.arange(ROWS)
    fits = r < NE * NE
    rb = np.zeros((ROWS, 96))
    rc = np.zeros((ROWS, 96))
    ra = np.zeros((NE * 8, 96))
    for t in range(3):
        rb[r[fits], t * 32 + r[fits] // NE] = 1
        rc[r[fits], t * 32 + r[fits] % NE] = 1
        ra[np.arange(NE * 8), t * 32 + np.arange(NE * 8) // 8] = 1
    inner = np.arange(1, 17)
    low, high = np.zeros(16, int), np.full(16, 17)
    jq = np.concatenate([np.repeat(inner, 16), low, high, inner, inner])
    kq = np.concatenate([np.tile(inner, 16), inner, inner, low, high])
    rj = np.zeros((RIM, 96))
    rk = np.zeros((RIM, 96))
    for t in range(3):
        rj[np.arange(RIM), t * 32 + jq] = 1
        rk[np.arange(RIM), t * 32 + kq] = 1
    cols = np.concatenate([np.arange(256), np.tile(np.arange(256, 320), 3)])
    qj = np.zeros((32, 512))
    qk = np.zeros((32, 512))
    qj[jq[cols], np.arange(448)] = 1
    qk[kq[cols], np.arange(448)] = 1
    qi = np.zeros((32, 512))
    c = np.arange(432)
    qi[(c % 144) // 8, c] = 1
    qb = np.zeros((32, 1024))
    qc = np.zeros((32, 1024))
    c = np.arange(1008)
    c = c[c % ROWS < NE * NE]
    qb[c % ROWS // NE, c] = 1
    qc[c % ROWS % NE, c] = 1
    flip = np.zeros((256, 256))
    n = np.arange(256)
    flip[n, n // 16 * 16 + 15 - n % 16] = 1
    left = np.concatenate([rb, rc, ra, rj, rk])
    right = np.concatenate([qj, qk, qi, qb[:, :512], qb[:, 512:], qc[:, :512], qc[:, 512:]])
    return left, right, flip


def split2(x):
    high = x.astype(BF)
    return high, (x - high.astype(F32)).astype(BF)


def split3(x):
    high = x.astype(BF)
    rest = x - high.astype(F32)
    middle = rest.astype(BF)
    return high, middle, (rest - middle.astype(F32)).astype(BF)


def dot(a, b):
    return jnp.dot(a, b, preferred_element_type=F32)


def widen(small, right):
    return sum(dot(term, right) for term in split3(small))


def deepen(left, small):
    return dot(left, jnp.concatenate(split3(small), axis=0))


def pick(condition):
    return jnp.where(condition, 1.0, 0.0).astype(BF)


def make_messages(planes, send, msgs):
    for axis in (2, 0, 1):
        count = 2 * COUNTS[axis]
        ids = send[axis : axis + 1, :] - 256 * axis
        chosen = pick(lax.broadcasted_iota(jnp.int32, (256, SLOTS), 0) == ids)
        high, low = split2(planes[axis])
        found = dot(high, chosen) + dot(low, chosen)
        msgs[STARTS[axis] : STARTS[axis] + count, :] = found.T[:count]


def list_rows(direction):
    axis, side = direction // 2, direction % 2
    return STARTS[axis] + side * COUNTS[axis], COUNTS[axis]


def greet(me):
    barrier = pltpu.get_barrier_semaphore()
    for offset in OFFSETS:
        pl.semaphore_signal(
            barrier, inc=1, device_id=(lax.rem(me + offset + 256, 256),), device_id_type=pl.DeviceIdType.MESH
        )
    pl.semaphore_wait(barrier, 6)


def start_copies(me, msgs, arrived, send_sem, recv_sem):
    copies = []
    for direction in (4, 5, 2, 3, 0, 1):
        start, count = list_rows(direction)
        copy = pltpu.make_async_remote_copy(
            src_ref=msgs.at[pl.ds(start, count)],
            dst_ref=arrived.at[pl.ds(start, count)],
            send_sem=send_sem.at[direction],
            recv_sem=recv_sem.at[direction],
            device_id=(lax.rem(me + OFFSETS[direction] + 256, 256),),
            device_id_type=pl.DeviceIdType.MESH,
        )
        copy.start()
        copies.append(copy)
    return copies


def reorient(planes, codes, flip):
    turned = jnp.concatenate([planes[16 * (15 - u) : 16 * (16 - u)] for u in range(16)], axis=0)
    planes = jnp.where(codes % 2 == 1, turned, planes)
    high, low = split2(planes)
    return jnp.where(codes >= 2, dot(flip, high) + dot(flip, low), planes)


def pair(table, axis):
    return jnp.concatenate([table[2 * axis : 2 * axis + 1, :], table[2 * axis + 1 : 2 * axis + 2, :]], axis=1)


def gather(axis, planes, arrived, nbr_src, nbr_idx, orient, flip):
    count = COUNTS[axis]
    src = pair(nbr_src, axis)
    idx = pair(nbr_idx, axis)
    codes = pair(orient, axis)
    here = jnp.where(src == 1, idx - 256 * axis, -1)
    there = jnp.where(src == 2 + 2 * axis, idx, jnp.where(src == 3 + 2 * axis, idx + count, -1))
    near = pick(lax.broadcasted_iota(jnp.int32, (256, 256), 0) == here)
    far = pick(lax.broadcasted_iota(jnp.int32, (2 * count, 256), 0) == there)
    high, low = split2(planes)
    far_high, far_low = split2(arrived[STARTS[axis] : STARTS[axis] + 2 * count, :].T)
    found = dot(high, near) + dot(low, near) + dot(far_high, far) + dot(far_low, far)
    return reorient(found, codes, flip)


def face_planes(field):
    side = [field[pl.ds(256, 256), :], field[pl.ds(14 * 256, 256), :]]
    middle = [
        jnp.concatenate([field[pl.ds(256 * i + 16 * j, 16), :] for i in range(16)], axis=0) for j in (1, 14)
    ]
    inner = [field[pl.ds(k, 256, stride=16), :] for k in (1, 14)]
    return [jnp.concatenate(both, axis=1) for both in (side, middle, inner)]


def exchange_field_kernel(field, send, arrived_out, msgs, arrived, send_sem, recv_sem):
    me = lax.axis_index("dev")
    make_messages(face_planes(field), send, msgs)
    greet(me)
    for copy in start_copies(me, msgs, arrived, send_sem, recv_sem):
        copy.wait()
    arrived_out[...] = arrived[...]


def exchange_rims_kernel(rims, send, arrived_out, msgs, arrived, send_sem, recv_sem):
    me = lax.axis_index("dev")
    make_messages([rims[axis] for axis in range(3)], send, msgs)
    greet(me)
    for copy in start_copies(me, msgs, arrived, send_sem, recv_sem):
        copy.wait()
    arrived_out[...] = arrived[...]


def make_operators(mats, turned, products, left, right, l1, l2, l4, l5, d12, d0):
    rb = left[0:336, :]
    rc = left[336:672, :]
    ra = left[672:816, :]
    rj = left[816:1136, :]
    rk = left[1136:1456, :]
    cols = lambda n: right[32 * n : 32 * n + 32, :]
    first = deepen(rb, widen(turned[1], cols(0))) * deepen(rc, widen(turned[2], cols(1)))
    high, low = split2(first)
    l1[:, 0:256] = high[:, 0:256]
    l1[:, 256:512] = high[:, 0:256]
    l1[:, 512:768] = low[:, 0:256]
    lane = lax.broadcasted_iota(jnp.int32, (ROWS, 256), 1)
    l1[:, 768:1024] = jnp.where(lane < 128, high[:, 256:].astype(F32), low[:, 256:].astype(F32)).astype(BF)
    lane = lax.broadcasted_iota(jnp.int32, (144, 512), 1)
    row = lax.broadcasted_iota(jnp.int32, (144, 512), 0)
    same = (lane & 7) == (row & 7)
    for mat, out in ((turned[0], l2), (mats[0], l4)):
        whole = jnp.where(same, deepen(ra, widen(mat, cols(2))), 0.0)
        high, low = split2(whole)
        out[...] = jnp.where(lane < 288, high.astype(F32), low.astype(F32)).astype(BF)
    for half in range(2):
        whole = deepen(rj, widen(mats[1], cols(3 + half))) * deepen(rk, widen(mats[2], cols(5 + half)))
        high, low = split2(whole)
        lane = lax.broadcasted_iota(jnp.int32, (RIM, 512), 1) + 512 * half
        l5[:, 512 * half : 512 * half + 512] = jnp.where(
            lane < 2 * ROWS, high.astype(F32), low.astype(F32)
        ).astype(BF)
    d12[...] = deepen(rb, products[1]) + deepen(rc, products[2])
    d0[...] = deepen(ra, products[0])


def solve_kernel(
    field, arrived, nbr_src, nbr_idx, orient, mats, turned, products, left, right, flip_in,
    solved, rims, l1, l2, l4, l5, d12, d0, ghosts, mid,
):
    make_operators(mats, turned, products, left, right, l1, l2, l4, l5, d12, d0)
    flip = flip_in[...]
    planes = face_planes(field)
    for axis in range(3):
        ghosts[axis] = gather(axis, planes[axis], arrived, nbr_src, nbr_idx, orient, flip)

    def forward_edges():
        high, low = split2(ghosts[0])
        out = dot(l1[:, 0:768], jnp.concatenate([high, low, high], axis=0))
        mid[0] = out[:, :SLOTS]
        mid[17] = out[:, SLOTS:]

    forward_edges()

    def forward(t):
        base = pl.multiple_of(512 * t, 512)
        x = jnp.concatenate([field[pl.ds(base, 256), :], field[pl.ds(base + 256, 256), :]], axis=1)
        high, low = split2(x)
        half = pl.multiple_of(32 * t, 32)
        rows = [ghosts[axis, pl.ds(half + 16 * n, 16), :] for axis in (1, 2) for n in (0, 1)]
        extra = jnp.concatenate(
            [
                jnp.concatenate([rows[n][:, :SLOTS], rows[n][:, SLOTS:], rows[n + 2][:, :SLOTS], rows[n + 2][:, SLOTS:]], axis=0)
                for n in (0, 1)
            ],
            axis=1,
        )
        g_high, g_low = split2(extra)
        data = jnp.concatenate([high, low, high, g_high, g_low, g_high, jnp.zeros((64, 256), BF)], axis=0)
        out = dot(l1[...], data)
        mid[2 * t + 1] = out[:, :SLOTS]
        mid[2 * t + 2] = out[:, SLOTS:]

    @pl.loop(0, 4)
    def _(t):
        forward(2 * t)
        forward(2 * t + 1)

    def middle(g):
        start = pl.multiple_of(16 * g, 16)
        block = mid[:, pl.ds(start, 16), :]
        y = jnp.concatenate([block[:, 0:8].reshape(144, SLOTS), block[:, 8:16].reshape(144, SLOTS)], axis=1)
        high, low = split2(y)
        z = dot(l2[:, 0:432], jnp.concatenate([high, low, high], axis=0))
        d = d12[pl.ds(start, 16), :]
        d = jnp.concatenate([d[0:8], d[8:16]], axis=1)
        base = d0[...]
        base = jnp.concatenate([base, base], axis=1)
        z = z / (base + jnp.concatenate([d] * NE, axis=0))
        high, low = split2(z)
        u = dot(l4[:, 0:432], jnp.concatenate([high, low, high], axis=0))
        mid[:, pl.ds(start, 8), :] = u[:, :SLOTS].reshape(NE, 8, SLOTS)
        mid[:, pl.ds(start + 8, 8), :] = u[:, SLOTS:].reshape(NE, 8, SLOTS)

    @pl.loop(0, 7)
    def _(g):
        for n in range(3):
            middle(3 * g + n)

    def spread(first, second):
        u = jnp.concatenate([mid[first], mid[second]], axis=1)
        high, low = split2(u)
        return jnp.concatenate([high, low, high, jnp.zeros((16, 256), BF)], axis=0)

    rims[0] = dot(l5[0:256, :], spread(0, 17))

    def inverse(t):
        out = dot(l5[...], spread(2 * t + 1, 2 * t + 2))
        base = pl.multiple_of(512 * t, 512)
        half = pl.multiple_of(32 * t, 32)
        for n in range(2):
            lanes = slice(SLOTS * n, SLOTS * n + SLOTS)
            solved[pl.ds(base + 256 * n, 256), :] = out[0:256, lanes]
            for axis in (1, 2):
                for side in (0, 1):
                    start = 256 + 32 * (axis - 1) + 16 * side
                    rims[axis, pl.ds(half + 16 * n, 16), SLOTS * side : SLOTS * side + SLOTS] = out[
                        start : start + 16, lanes
                    ]

    @pl.loop(0, 4)
    def _(t):
        inverse(2 * t)
        inverse(2 * t + 1)


def finish_kernel(solved, rims, arrived, nbr_src, nbr_idx, orient, flip_in, out, back):
    flip = flip_in[...]
    for axis in range(3):
        back[axis] = gather(axis, rims[axis], arrived, nbr_src, nbr_idx, orient, flip)
    rank = lax.broadcasted_iota(jnp.int32, (16, 16, SLOTS), 1)

    @pl.loop(0, 16)
    def _(i):
        base = pl.multiple_of(256 * i, 256)
        half = pl.multiple_of(16 * i, 16)
        inner = back[2, pl.ds(half, 16), :]
        low = jnp.broadcast_to(inner[:, None, :SLOTS], (16, 16, SLOTS))
        high = jnp.broadcast_to(inner[:, None, SLOTS:], (16, 16, SLOTS))
        added = jnp.where(rank == 1, low, jnp.where(rank == 14, high, 0.0)).reshape(256, SLOTS)
        out[pl.ds(base, 256), :] = solved[pl.ds(base, 256), :] + added
        out[pl.ds(base + 16, 16), :] += back[1, pl.ds(half, 16), :SLOTS]
        out[pl.ds(base + 224, 16), :] += back[1, pl.ds(half, 16), SLOTS:]

    out[256:512, :] += back[0, :, :SLOTS]
    out[14 * 256 : 15 * 256, :] += back[0, :, SLOTS:]


def exchange(kernel, planes, send, name, number):
    return pl.pallas_call(
        kernel,
        out_shape=jax.ShapeDtypeStruct((192, 256), F32),
        in_specs=[VMEM] * 2,
        out_specs=VMEM,
        scratch_shapes=[
            pltpu.VMEM((192, 256), F32),
            pltpu.VMEM((192, 256), F32),
            pltpu.SemaphoreType.DMA((6,)),
            pltpu.SemaphoreType.DMA((6,)),
        ],
        compiler_params=pltpu.CompilerParams(collective_id=number, has_side_effects=True),
        name=name,
    )(planes, send)


def shards(field, s_mats, lam, coeff, nbr_src, nbr_idx, orient, send_x, send_y, send_z):
    left, right, flip = (jnp.asarray(table, BF) for table in make_tables())
    flat = field.reshape(4096, SLOTS)
    mats = jnp.pad(s_mats, ((0, 0), (0, 14), (0, 14)))
    turned = jnp.swapaxes(mats, 1, 2)
    products = jnp.pad(lam[:, :, None] * coeff[:, None, :], ((0, 0), (0, 14), (0, 0)))
    blank = ((0, 0), (0, 96))
    send = jnp.concatenate(
        [
            jnp.pad(send_x.reshape(1, 32), blank, constant_values=-1),
            jnp.pad(send_y.reshape(1, 32), blank, constant_values=-1),
            send_z.reshape(1, SLOTS),
        ],
        axis=0,
    )
    arrived = exchange(exchange_field_kernel, flat, send, "exchange_field", 0)
    solved, rims = pl.pallas_call(
        solve_kernel,
        out_shape=(jax.ShapeDtypeStruct((4096, SLOTS), F32), jax.ShapeDtypeStruct((3, 256, 256), F32)),
        in_specs=[VMEM] * 11,
        out_specs=(VMEM, VMEM),
        scratch_shapes=[
            pltpu.VMEM((ROWS, 1024), BF),
            pltpu.VMEM((144, 512), BF),
            pltpu.VMEM((144, 512), BF),
            pltpu.VMEM((RIM, 1024), BF),
            pltpu.VMEM((ROWS, SLOTS), F32),
            pltpu.VMEM((144, SLOTS), F32),
            pltpu.VMEM((3, 256, 256), F32),
            pltpu.VMEM((NE, ROWS, SLOTS), F32),
        ],
        name="solve",
    )(flat, arrived, nbr_src, nbr_idx, orient, mats, turned, products, left, right, flip)
    returned = exchange(exchange_rims_kernel, rims, send, "exchange_rims", 1)
    out = pl.pallas_call(
        finish_kernel,
        out_shape=jax.ShapeDtypeStruct((4096, SLOTS), F32),
        in_specs=[VMEM] * 7,
        out_specs=VMEM,
        scratch_shapes=[pltpu.VMEM((3, 256, 256), F32)],
        name="finish",
    )(solved, rims, returned, nbr_src, nbr_idx, orient, flip)
    return out.reshape(field.shape)


def solution(mesh):
    placed = (
        P(None, None, None, "dev"),
        P(),
        P(),
        P(None, "dev"),
        P(None, "dev"),
        P(None, "dev"),
        P(None, "dev"),
        P(None, "dev"),
        P(None, "dev"),
        P(None, "dev"),
    )
    return jax.shard_map(
        shards, mesh=mesh, in_specs=placed, out_specs=P(None, None, None, "dev"), check_vma=False
    )
```

profile of v0, /device:TPU:1, one launch (start us, length us, event | category | flops | bytes accessed | tf_op | source)
XLA Modules:
  0.0 57.7 jit_solution(16706858353705205253)
XLA Ops:
  0.0 0.8 %reshape.18 = s32[1,32]{1,0:T(1,128)S(1)} reshape(s32[2,16]{1,0:T(2,128)} %param.20) | data formatting | bytes 256 | tf_op jit(solution)/shard_map/reshape | solution.py:357
  0.8 0.8 %reshape.19 = s32[1,32]{1,0:T(1,128)S(1)} reshape(s32[2,16]{1,0:T(2,128)} %param.21) | data formatting | bytes 256 | tf_op jit(solution)/shard_map/reshape | solution.py:358
  1.5 0.8 %reshape.20 = s32[1,128]{1,0:T(1,128)S(1)} reshape(s32[2,64]{1,0:T(2,128)} %param.22) | data formatting | bytes 1024 | tf_op jit(solution)/shard_map/reshape | solution.py:359
  2.3 0.6 %fusion.send = s32[3,128]{1,0:T(4,128)} fusion(s32[1,32]{1,0:T(1,128)S(1)} %reshape.19, s32[1,32]{1,0:T(1,128)S(1)} %reshape.18, s32[1,128]{1,0:T(1,128)S(1)} %reshape.20), kind=kLoop, calls=%fused_computation.5 | loop fusion | flops 3072 | bytes 2304 | tf_op jit(solution)/shard_map/concatenate | solution.py:355
  2.9 0.9 %copy.14 = f32[3,18,18]{1,2,0:T(8,128)S(1)} copy(f32[3,18,18]{2,1,0:T(8,128)} %param.14) | data formatting | bytes 7776 | tf_op args[1]
  3.7 0.1 copy.16
  3.9 0.6 %pad_bitcast_fusion.turned = f32[3,32,32]{2,1,0:T(8,128)} fusion(f32[3,18,18]{1,2,0:T(8,128)S(1)} %copy.14), kind=kLoop, calls=%fused_computation.1 | loop fusion | bytes 16176 | tf_op jit(solution)/shard_map/transpose | solution.py:352
  4.5 0.6 %pad.17.clone.mats = f32[3,32,32]{2,1,0:T(8,128)} pad(f32[3,18,18]{2,1,0:T(8,128)S(1)} %copy.16, f32[]{:T(128)} %constant.10.clone.1), padding=0_0x0_14x0_14 | pad | bytes 16180 | tf_op jit(solution)/shard_map/jit(_pad)/pad | solution.py:351
  5.1 0.8 %broadcast_multiply_fusion = f32[3,18,128]{2,1,0:T(8,128)S(1)} fusion(f32[3,128]{1,0:T(4,128)} %param.16, f32[3,18]{1,0:T(4,128)} %param.15), kind=kLoop, calls=%fused_computation | loop fusion | flops 6912 | bytes 29400 | tf_op jit(solution)/shard_map/mul | solution.py:353
  5.9 0.6 %pad.18.products = f32[3,32,128]{2,1,0:T(8,128)} pad(f32[3,18,128]{2,1,0:T(8,128)S(1)} %broadcast_multiply_fusion, f32[]{:T(128)} %constant.10.clone.1), padding=0_0x0_14x0_0 | pad | bytes 76804 | tf_op jit(solution)/shard_map/jit(_pad)/pad | solution.py:353
  6.5 17.8 %exchange_field.1.arrived = f32[192,256]{1,0:T(8,128)} custom-call(f32[4096,128]{1,0:T(8,128)} %bitcast.4, s32[3,128]{1,0:T(4,128)} %fusion.send), custom_call_target="tpu_custom_call" | custom-call | tf_op jit(solution)/shard_map/exchange_field/pallas_call | solution.py:332
  24.3 15.6 %solve.1 = (f32[4096,128]{1,0:T(8,128)}, f32[3,256,256]{2,1,0:T(8,128)}) custom-call(f32[4096,128]{1,0:T(8,128)} %bitcast.5, f32[192,256]{1,0:T(8,128)} %exchange_field.1.arrived, s32[6,128]{1,0:T(8,128)} %nbr_src.3, s32[6,128]{1,0:T(8,128)} %nbr_idx.3, s32[6,128]{1,0:T(8,128)} %orient.3, f32[3,32,32]{2,1,0:T(8,128)} %pad.17.clone.mats, ...), custom_call_target="tpu_custom_call" | custom-call | tf_op jit(solution)/shard_map/solve/pallas_call | solution.py:364
  39.9 12.4 %exchange_rims.1.arrived = f32[192,256]{1,0:T(8,128)} custom-call(f32[3,256,256]{2,1,0:T(8,128)} %get-tuple-element.8.rims, s32[3,128]{1,0:T(4,128)} %fusion.send), custom_call_target="tpu_custom_call" | custom-call | tf_op jit(solution)/shard_map/exchange_rims/pallas_call | solution.py:332
  52.3 5.5 %finish.1 = f32[4096,128]{1,0:T(8,128)} custom-call(f32[4096,128]{1,0:T(8,128)} %get-tuple-element.7.solved, f32[3,256,256]{2,1,0:T(8,128)} %get-tuple-element.8.rims, f32[192,256]{1,0:T(8,128)} %exchange_rims.1.arrived, s32[6,128]{1,0:T(8,128)} %nbr_src.3, s32[6,128]{1,0:T(8,128)} %nbr_idx.3, s32[6,128]{1,0:T(8,128)} %orient.3, ...), custom_call_target="tpu_custom_call" | custom-call | tf_op jit(solution)/shard_map/finish/pallas_call | solution.py:382
where the time goes:
time: 58 us; the launch traced here: 57.7 us
  Pallas kernels  51.2 us (88%)
  local copies, waits for them, and re-layouts  5.12 us (9%)
  other arithmetic  1.37 us (2%)
    pallas_call x2, Pallas kernels, exchange(): pl.pallas_call(kernel, out_shape=jax.ShapeDtypeStruct((192, 256), F32), i...  30.2 us
    pallas_call x1, Pallas kernels, shards(): pl.pallas_call(solve_kernel, out_shape=(jax.ShapeDtypeStruct((4096, SLOTS...  15.6 us
    pallas_call x1, Pallas kernels, shards(): pl.pallas_call(finish_kernel, out_shape=jax.ShapeDtypeStruct((4096, SLOTS...  5.45 us

commit v1 on v0

v1 whole, which is shorter than its diff:
```python
import functools

import jax
import jax.numpy as jnp
import numpy as np
from jax import lax
from jax.experimental import pallas as pl
from jax.experimental.pallas import tpu as pltpu
from jax.sharding import PartitionSpec as P

NP = 16
NE = 18
SLOTS = 128
ROWS = 336
RIM = 320
COUNTS = (16, 16, 64)
STARTS = (0, 32, 64)
OFFSETS = (-1, 1, -4, 4, -16, 16)
BF = jnp.bfloat16
F32 = jnp.float32
VMEM = pl.BlockSpec(memory_space=pltpu.VMEM)


def make_tables():
    r = np.arange(ROWS)
    fits = r < NE * NE
    rb = np.zeros((ROWS, 96))
    rc = np.zeros((ROWS, 96))
    ra = np.zeros((NE * 8, 96))
    for t in range(3):
        rb[r[fits], t * 32 + r[fits] // NE] = 1
        rc[r[fits], t * 32 + r[fits] % NE] = 1
        ra[np.arange(NE * 8), t * 32 + np.arange(NE * 8) // 8] = 1
    inner = np.arange(1, 17)
    low, high = np.zeros(16, int), np.full(16, 17)
    jq = np.concatenate([np.repeat(inner, 16), low, high, inner, inner])
    kq = np.concatenate([np.tile(inner, 16), inner, inner, low, high])
    rj = np.zeros((RIM, 96))
    rk = np.zeros((RIM, 96))
    for t in range(3):
        rj[np.arange(RIM), t * 32 + jq] = 1
        rk[np.arange(RIM), t * 32 + kq] = 1
    cols = np.concatenate([np.arange(256), np.tile(np.arange(256, 320), 3)])
    qj = np.zeros((32, 512))
    qk = np.zeros((32, 512))
    qj[jq[cols], np.arange(448)] = 1
    qk[kq[cols], np.arange(448)] = 1
    qi = np.zeros((32, 512))
    c = np.arange(432)
    qi[(c % 144) // 8, c] = 1
    qb = np.zeros((32, 1024))
    qc = np.zeros((32, 1024))
    c = np.arange(1008)
    c = c[c % ROWS < NE * NE]
    qb[c % ROWS // NE, c] = 1
    qc[c % ROWS % NE, c] = 1
    left = np.concatenate([rb, rc, ra, rj, rk])
    right = np.concatenate([qj, qk, qi, qb[:, :512], qb[:, 512:], qc[:, :512], qc[:, 512:]])
    return left, right


def split2(x):
    high = x.astype(BF)
    return high, (x - high.astype(F32)).astype(BF)


def split3(x):
    high = x.astype(BF)
    rest = x - high.astype(F32)
    middle = rest.astype(BF)
    return high, middle, (rest - middle.astype(F32)).astype(BF)


def dot(a, b):
    return jnp.dot(a, b, preferred_element_type=F32)


def widen(small, right):
    return sum(dot(term, right) for term in split3(small))


def deepen(left, small):
    return dot(left, jnp.concatenate(split3(small), axis=0))


def pick(condition):
    return jnp.where(condition, 1.0, 0.0).astype(BF)


def list_rows(direction):
    axis, side = direction // 2, direction % 2
    return STARTS[axis] + side * COUNTS[axis], COUNTS[axis]


def find_neighbours(me):
    spot = (lax.rem(me, 4), lax.rem(lax.div(me, 4), 4), lax.div(me, 16))
    tops = (3, 3, 15)
    return [spot[d // 2] > 0 if d % 2 == 0 else spot[d // 2] < tops[d // 2] for d in range(6)]


def greet(me, present):
    barrier = pltpu.get_barrier_semaphore()
    for direction in range(6):

        @pl.when(present[direction])
        def _():
            pl.semaphore_signal(
                barrier, inc=1, device_id=(me + OFFSETS[direction],), device_id_type=pl.DeviceIdType.MESH
            )

    return barrier


def outgoing(me, direction, msgs, arrived, send_sem, recv_sem):
    start, count = list_rows(direction)
    return pltpu.make_async_remote_copy(
        src_ref=msgs.at[pl.ds(start, count)],
        dst_ref=arrived.at[pl.ds(start, count)],
        send_sem=send_sem.at[direction],
        recv_sem=recv_sem.at[direction],
        device_id=(me + OFFSETS[direction],),
        device_id_type=pl.DeviceIdType.MESH,
    )


def send_axis(axis, me, present, parts, send, msgs, arrived, send_sem, recv_sem):
    count = 2 * COUNTS[axis]
    ids = send[axis : axis + 1, :] - 256 * axis
    chosen = pick(lax.broadcasted_iota(jnp.int32, (256, SLOTS), 0) == ids)
    found = dot(parts[axis, 0], chosen) + dot(parts[axis, 1], chosen)
    msgs[STARTS[axis] : STARTS[axis] + count, :] = found.T[:count]


def launch(axis, me, present, msgs, arrived, send_sem, recv_sem):
    for direction in (2 * axis, 2 * axis + 1):

        @pl.when(present[direction])
        def _():
            outgoing(me, direction, msgs, arrived, send_sem, recv_sem).start()


def await_axis(axis, me, present, msgs, arrived, send_sem, recv_sem):
    for direction in (2 * axis, 2 * axis + 1):

        @pl.when(present[direction])
        def _():
            outgoing(me, direction, msgs, arrived, send_sem, recv_sem).wait_send()

        @pl.when(present[direction ^ 1])
        def _():
            outgoing(me, direction, msgs, arrived, send_sem, recv_sem).wait_recv()


def pair(table, axis):
    return jnp.concatenate([table[2 * axis : 2 * axis + 1, :], table[2 * axis + 1 : 2 * axis + 2, :]], axis=1)


def gather_near(axis, parts, found, nbr_src, nbr_idx):
    src = pair(nbr_src, axis)
    idx = pair(nbr_idx, axis)
    here = jnp.where(src == 1, idx - 256 * axis, -1)
    near = pick(lax.broadcasted_iota(jnp.int32, (256, 256), 0) == here)
    found[axis] = dot(parts[axis, 0], near) + dot(parts[axis, 1], near)


def gather_far(axis, arrived, found, out, nbr_src, nbr_idx, orient):
    count = COUNTS[axis]
    src = pair(nbr_src, axis)
    idx = pair(nbr_idx, axis)
    codes = pair(orient, axis)
    there = jnp.where(src == 2 + 2 * axis, idx, jnp.where(src == 3 + 2 * axis, idx + count, -1))
    far = pick(lax.broadcasted_iota(jnp.int32, (2 * count, 256), 0) == there)
    high, low = split2(arrived[STARTS[axis] : STARTS[axis] + 2 * count, :].T)
    found[axis] += dot(high, far) + dot(low, far)
    first = codes % 2 == 1
    second = codes >= 2
    back = 7 - lax.broadcasted_iota(jnp.int32, (8, SLOTS), 0)
    for lanes in (slice(0, SLOTS), slice(SLOTS, 2 * SLOTS)):
        for u in range(16):
            rows = [
                jnp.where(
                    first[:, lanes],
                    found[axis, 16 * (15 - u) + 8 * n : 16 * (15 - u) + 8 * n + 8, lanes],
                    found[axis, 16 * u + 8 * n : 16 * u + 8 * n + 8, lanes],
                )
                for n in (0, 1)
            ]
            for n in (0, 1):
                turned = jnp.take_along_axis(rows[1 - n], back, axis=0)
                out[axis, 16 * u + 8 * n : 16 * u + 8 * n + 8, lanes] = jnp.where(second[:, lanes], turned, rows[n])


def face_planes(axis, field):
    if axis == 0:
        both = [field[256:512, :], field[14 * 256 : 15 * 256, :]]
    elif axis == 1:
        both = [
            jnp.concatenate([field[256 * i + 16 * j : 256 * i + 16 * j + 16, :] for i in range(16)], axis=0)
            for j in (1, 14)
        ]
    else:
        both = [field[pl.ds(k, 256, stride=16), :] for k in (1, 14)]
    return jnp.concatenate(both, axis=1)


def product_blocks(rows, depth, left_a, left_b, small_a, small_b, columns):
    split_a = jnp.concatenate(split3(small_a), axis=0)
    split_b = jnp.concatenate(split3(small_b), axis=0)
    for start in range(0, rows, depth):
        piece = slice(start, start + depth)
        yield piece, dot(left_a[piece, :], split_a[:, columns]) * dot(left_b[piece, :], split_b[:, columns])


def make_operators(s_mats, lam, coeff, left, right, l1, l2, l4, l5, d12, d0):
    rb = left.at[0:336]
    rc = left.at[336:672]
    ra = left.at[672:816]
    rj = left.at[816:1136]
    rk = left.at[1136:1456]
    cols = lambda n: right[32 * n : 32 * n + 32, :]
    room = ((0, 14), (0, 14))
    mats = [jnp.pad(s_mats[axis], room) for axis in range(3)]
    turned = [jnp.pad(s_mats[axis].T, room) for axis in range(3)]
    small = widen(turned[1], cols(0)), widen(turned[2], cols(1))
    for piece, block in product_blocks(ROWS, 112, rb, rc, *small, slice(0, 256)):
        high, low = split2(block)
        l1[piece, 0:256] = high
        l1[piece, 256:512] = high
        l1[piece, 512:768] = low
    lane = lax.broadcasted_iota(jnp.int32, (112, 256), 1)
    for piece, block in product_blocks(ROWS, 112, rb, rc, *small, slice(256, 512)):
        high, low = split2(block)
        l1[piece, 768:1024] = jnp.where(lane < 128, high.astype(F32), low.astype(F32)).astype(BF)
    lane = lax.broadcasted_iota(jnp.int32, (144, 256), 1)
    row = lax.broadcasted_iota(jnp.int32, (144, 256), 0)
    same = (lane & 7) == (row & 7)
    for mat, out in ((turned[0], l2), (mats[0], l4)):
        whole = jnp.concatenate(split3(widen(mat, cols(2))), axis=0)
        for half in range(2):
            columns = slice(256 * half, 256 * half + 256)
            high, low = split2(jnp.where(same, dot(ra[...], whole[:, columns]), 0.0))
            out[:, columns] = jnp.where(lane < 288 - 256 * half, high.astype(F32), low.astype(F32)).astype(BF)
    lane = lax.broadcasted_iota(jnp.int32, (80, 256), 1)
    for half in range(2):
        small = widen(mats[1], cols(3 + half)), widen(mats[2], cols(5 + half))
        for part in range(2):
            base = 512 * half + 256 * part
            for piece, block in product_blocks(RIM, 80, rj, rk, *small, slice(256 * part, 256 * part + 256)):
                high, low = split2(block)
                l5[piece, base : base + 256] = jnp.where(
                    lane < 2 * ROWS - base, high.astype(F32), low.astype(F32)
                ).astype(BF)
    levels = jnp.pad(lam[...], ((0, 5), (0, 110))).T[:32]
    products = [levels[:, axis : axis + 1] * coeff[axis : axis + 1, :] for axis in range(3)]
    d12[...] = deepen(rb[...], products[1]) + deepen(rc[...], products[2])
    d0[...] = deepen(ra[...], products[0])


def smooth_kernel(
    field_in, s_mats_in, lam_in, coeff_in, src_in, idx_in, orient_in, send_x_in, send_y_in, send_z_in, left_in, right_in,
    solved_out, back_out,
    field, s_mats, lam, coeff, nbr_src, nbr_idx, orient, send_x, send_y, send_z, left, right,
    l1, l2, l4, l5, d12, d0, send, parts, found, ghosts, mid, solved,
    msgs, arrived, load_sem, store_sem, send_sem, recv_sem,
):
    me = lax.axis_index("dev")
    loads = [
        pltpu.make_async_copy(source, target, load_sem.at[n])
        for n, (source, target) in enumerate(
            (
                (field_in, field), (send_x_in, send_x), (send_y_in, send_y), (send_z_in, send_z),
                (left_in, left), (right_in, right), (s_mats_in, s_mats), (lam_in, lam), (coeff_in, coeff),
                (src_in, nbr_src), (idx_in, nbr_idx), (orient_in, orient),
            )
        )
    ]
    for load in loads:
        load.start()
    present = find_neighbours(me)
    for direction in range(6):
        start, count = list_rows(direction)

        @pl.when(jnp.logical_not(present[direction ^ 1]))
        def _():
            for phase in range(2):
                arrived[phase, start : start + count, :] = jnp.zeros((count, 256), F32)

    barrier = greet(me, present)
    for load in loads[:4]:
        load.wait()
    send[...] = jnp.full((8, SLOTS), -1, jnp.int32)
    send[0:1, 0:16] = send_x[0:1, :]
    send[0:1, 16:32] = send_x[1:2, :]
    send[1:2, 0:16] = send_y[0:1, :]
    send[1:2, 16:32] = send_y[1:2, :]
    send[2:3, 0:64] = send_z[0:1, :]
    send[2:3, 64:128] = send_z[1:2, :]

    wires = [(me, present, msgs, arrived.at[n], send_sem.at[n], recv_sem.at[n]) for n in range(2)]

    def send_planes(axis, wire):
        send_axis(axis, *wire[:2], parts, send, *wire[2:])

    for axis in (2, 0, 1):
        parts[axis, 0], parts[axis, 1] = split2(face_planes(axis, field))
        send_planes(axis, wires[0])
        if axis == 2:
            total = sum(jnp.where(flag, 1, 0) for flag in present)
            pl.semaphore_wait(barrier, total)
        launch(axis, *wires[0])

    for load in loads[4:]:
        load.wait()
    make_operators(s_mats, lam, coeff, left, right, l1, l2, l4, l5, d12, d0)
    for axis in range(3):
        gather_near(axis, parts, found, nbr_src, nbr_idx)

    def forward_inner(t):
        base = pl.multiple_of(512 * t, 512)
        x = jnp.concatenate([field[pl.ds(base, 256), :], field[pl.ds(base + 256, 256), :]], axis=1)
        high, low = split2(x)
        out = dot(l1[:, 0:768], jnp.concatenate([high, low, high], axis=0))
        mid[2 * t + 1] = out[:, :SLOTS]
        mid[2 * t + 2] = out[:, SLOTS:]

    @pl.loop(0, 4)
    def _(t):
        forward_inner(2 * t)
        forward_inner(2 * t + 1)

    for axis in (0, 1, 2):
        await_axis(axis, *wires[0])
        gather_far(axis, arrived.at[0], found, ghosts, nbr_src, nbr_idx, orient)

    high, low = split2(ghosts[0])
    out = dot(l1[:, 0:768], jnp.concatenate([high, low, high], axis=0))
    mid[0] = out[:, :SLOTS]
    mid[17] = out[:, SLOTS:]

    def forward_outer(t):
        half = pl.multiple_of(32 * t, 32)
        extra = jnp.concatenate(
            [
                jnp.concatenate(
                    [
                        ghosts[axis, pl.ds(half + 16 * n, 16), SLOTS * side : SLOTS * side + SLOTS]
                        for axis in (1, 2)
                        for side in (0, 1)
                    ],
                    axis=0,
                )
                for n in (0, 1)
            ],
            axis=1,
        )
        high, low = split2(extra)
        out = dot(l1[:, 768:960], jnp.concatenate([high, low, high], axis=0))
        mid[2 * t + 1] += out[:, :SLOTS]
        mid[2 * t + 2] += out[:, SLOTS:]

    @pl.loop(0, 4)
    def _(t):
        forward_outer(2 * t)
        forward_outer(2 * t + 1)

    def middle(g):
        start = pl.multiple_of(16 * g, 16)
        block = mid[:, pl.ds(start, 16), :]
        y = jnp.concatenate([block[:, 0:8].reshape(144, SLOTS), block[:, 8:16].reshape(144, SLOTS)], axis=1)
        high, low = split2(y)
        z = dot(l2[:, 0:432], jnp.concatenate([high, low, high], axis=0))
        d = d12[pl.ds(start, 16), :]
        d = jnp.concatenate([d[0:8], d[8:16]], axis=1)
        base = d0[...]
        base = jnp.concatenate([base, base], axis=1)
        z = z / (base + jnp.concatenate([d] * NE, axis=0))
        high, low = split2(z)
        u = dot(l4[:, 0:432], jnp.concatenate([high, low, high], axis=0))
        mid[:, pl.ds(start, 8), :] = u[:, :SLOTS].reshape(NE, 8, SLOTS)
        mid[:, pl.ds(start + 8, 8), :] = u[:, SLOTS:].reshape(NE, 8, SLOTS)

    @pl.loop(0, 7)
    def _(g):
        for n in range(3):
            middle(3 * g + n)

    def spread(first, second):
        u = jnp.concatenate([mid[first], mid[second]], axis=1)
        high, low = split2(u)
        return jnp.concatenate([high, low, high, jnp.zeros((16, 256), BF)], axis=0)

    parts[0, 0], parts[0, 1] = split2(dot(l5[0:256, :], spread(0, 17)))
    send_planes(0, wires[1])
    launch(0, *wires[1])

    def store(t):
        rows = pl.ds(pl.multiple_of(512 * t, 512), 512)
        return pltpu.make_async_copy(solved.at[rows], solved_out.at[rows], store_sem.at[t])

    def inverse(t):
        out = dot(l5[...], spread(2 * t + 1, 2 * t + 2))
        base = pl.multiple_of(512 * t, 512)
        half = pl.multiple_of(32 * t, 32)
        for n in range(2):
            lanes = slice(SLOTS * n, SLOTS * n + SLOTS)
            solved[pl.ds(base + 256 * n, 256), :] = out[0:256, lanes]
            for axis in (1, 2):
                for side in (0, 1):
                    start = 256 + 32 * (axis - 1) + 16 * side
                    high, low = split2(out[start : start + 16, lanes])
                    rows = pl.ds(half + 16 * n, 16)
                    parts[axis, 0, rows, SLOTS * side : SLOTS * side + SLOTS] = high
                    parts[axis, 1, rows, SLOTS * side : SLOTS * side + SLOTS] = low

    @pl.loop(0, 4)
    def _(t):
        inverse(2 * t)
        inverse(2 * t + 1)

    for axis in (2, 1):
        send_planes(axis, wires[1])
        launch(axis, *wires[1])
    for t in range(8):
        store(t).start()
    for axis in range(3):
        gather_near(axis, parts, found, nbr_src, nbr_idx)
    for axis in (0, 1, 2):
        await_axis(axis, *wires[1])
        gather_far(axis, arrived.at[1], found, back_out, nbr_src, nbr_idx, orient)
    for t in range(8):
        store(t).wait()


def finish_kernel(solved, back, out):
    step = pl.program_id(0)
    rank = lax.broadcasted_iota(jnp.int32, (16, 16, SLOTS), 1)
    for n in range(2):
        half = pl.multiple_of(32 * step + 16 * n, 16)
        base = 256 * n
        inner = back[2, pl.ds(half, 16), :]
        low = jnp.broadcast_to(inner[:, None, :SLOTS], (16, 16, SLOTS))
        high = jnp.broadcast_to(inner[:, None, SLOTS:], (16, 16, SLOTS))
        added = jnp.where(rank == 1, low, jnp.where(rank == 14, high, 0.0)).reshape(256, SLOTS)
        out[base : base + 256, :] = solved[base : base + 256, :] + added
        out[base + 16 : base + 32, :] += back[1, pl.ds(half, 16), :SLOTS]
        out[base + 224 : base + 240, :] += back[1, pl.ds(half, 16), SLOTS:]

    @pl.when(step == 0)
    def _():
        out[256:512, :] += back[0, :, :SLOTS]

    @pl.when(step == 7)
    def _():
        out[0:256, :] += back[0, :, SLOTS:]


def shards(field, s_mats, lam, coeff, nbr_src, nbr_idx, orient, send_x, send_y, send_z):
    left, right = (jnp.asarray(table, BF) for table in make_tables())
    flat = field.reshape(4096, SLOTS)
    inputs = (flat, s_mats, lam, coeff, nbr_src, nbr_idx, orient, send_x, send_y, send_z, left, right)
    solved, back = pl.pallas_call(
        smooth_kernel,
        out_shape=(jax.ShapeDtypeStruct((4096, SLOTS), F32), jax.ShapeDtypeStruct((3, 256, 256), F32)),
        in_specs=[pl.BlockSpec(memory_space=pl.ANY)] * 12,
        out_specs=(pl.BlockSpec(memory_space=pl.ANY), VMEM),
        scratch_shapes=[pltpu.VMEM(value.shape, value.dtype) for value in inputs]
        + [
            pltpu.VMEM((ROWS, 1024), BF),
            pltpu.VMEM((144, 512), BF),
            pltpu.VMEM((144, 512), BF),
            pltpu.VMEM((RIM, 1024), BF),
            pltpu.VMEM((ROWS, SLOTS), F32),
            pltpu.VMEM((144, SLOTS), F32),
            pltpu.VMEM((8, SLOTS), jnp.int32),
            pltpu.VMEM((3, 2, 256, 256), BF),
            pltpu.VMEM((3, 256, 256), F32),
            pltpu.VMEM((3, 256, 256), F32),
            pltpu.VMEM((NE, ROWS, SLOTS), F32),
            pltpu.VMEM((4096, SLOTS), F32),
            pltpu.VMEM((192, 256), F32),
            pltpu.VMEM((2, 192, 256), F32),
            pltpu.SemaphoreType.DMA((12,)),
            pltpu.SemaphoreType.DMA((8,)),
            pltpu.SemaphoreType.DMA((2, 6)),
            pltpu.SemaphoreType.DMA((2, 6)),
        ],
        compiler_params=pltpu.CompilerParams(collective_id=0, has_side_effects=True),
        name="smooth",
    )(*inputs)
    whole = lambda step: (0, 0, 0)
    some = pl.BlockSpec((512, SLOTS), lambda step: (step, 0))
    out = pl.pallas_call(
        finish_kernel,
        out_shape=jax.ShapeDtypeStruct((4096, SLOTS), F32),
        grid=(8,),
        in_specs=[some, pl.BlockSpec((3, 256, 256), whole)],
        out_specs=some,
        name="finish",
    )(solved, back)
    return out.reshape(field.shape)


def solution(mesh):
    placed = (
        P(None, None, None, "dev"),
        P(),
        P(),
        P(None, "dev"),
        P(None, "dev"),
        P(None, "dev"),
        P(None, "dev"),
        P(None, "dev"),
        P(None, "dev"),
        P(None, "dev"),
    )
    return jax.shard_map(
        shards, mesh=mesh, in_specs=placed, out_specs=P(None, None, None, "dev"), check_vma=False
    )
```

time: 58 us -> 32.6 us (0.56)
  the two profiles are of different devices: /device:TPU:1 before, /device:TPU:6 now
where the time goes in v1:
time: 32.6 us; the launch traced here: 32.3 us
  Pallas kernels  32.3 us (99%)
    pallas_call x1, Pallas kernels, shards(): pl.pallas_call(smooth_kernel, out_shape=(jax.ShapeDtypeStruct((4096, SLOT...  26.2 us
    pallas_call x1, Pallas kernels, shards(): pl.pallas_call(finish_kernel, out_shape=jax.ShapeDtypeStruct((4096, SLOTS...  6.07 us

profile of v1, /device:TPU:6, one launch (start us, length us, event | category | flops | bytes accessed | tf_op | source)
XLA Modules:
  0.0 32.3 jit_solution(15402717186194639414)
XLA Ops:
  0.0 26.2 %smooth.1 = (f32[4096,128]{1,0:T(8,128)}, f32[3,256,256]{2,1,0:T(8,128)}) custom-call(f32[4096,128]{1,0:T(8,128)} %bitcast.2, f32[3,18,18]{2,1,0:T(8,128)} %s_mats_in.1, f32[3,18]{1,0:T(4,128)} %lam_in.1, f32[3,128]{1,0:T(4,128)} %coeff_in.1, s32[6,128]{1,0:T(8,128)} %src_in.1, s32[6,128]{1,0:T(8,128)} %idx_in.1, s32[6,128]{1,0:T(8,128)} %orient_in.1, ...), custom_call_target="tpu_custom_call" | custom-call | tf_op jit(solution)/shard_map/smooth/pallas_call | solution.py:461
  26.3 6.1 %finish.1 = f32[4096,128]{1,0:T(8,128)} custom-call(f32[4096,128]{1,0:T(8,128)} %get-tuple-element.7.solved, f32[3,256,256]{2,1,0:T(8,128)} %get-tuple-element.8.back), custom_call_target="tpu_custom_call" | custom-call | tf_op jit(solution)/shard_map/finish/pallas_call | solution.py:492

commit v2 on v1

--- a/solution.py
+++ b/solution.py
@@ -85,6 +85,10 @@
 
 def pick(condition):
     return jnp.where(condition, 1.0, 0.0).astype(BF)
+
+
+def aligned(index, step):
+    return index if isinstance(index, int) else pl.multiple_of(index, step)
 
 
 def list_rows(direction):
@@ -258,10 +262,10 @@
 
 def smooth_kernel(
     field_in, s_mats_in, lam_in, coeff_in, src_in, idx_in, orient_in, send_x_in, send_y_in, send_z_in, left_in, right_in,
-    solved_out, back_out,
+    solved,
     field, s_mats, lam, coeff, nbr_src, nbr_idx, orient, send_x, send_y, send_z, left, right,
-    l1, l2, l4, l5, d12, d0, send, parts, found, ghosts, mid, solved,
-    msgs, arrived, load_sem, store_sem, send_sem, recv_sem,
+    l1, l2, l4, l5, d12, d0, send, parts, found, ghosts, mid,
+    msgs, arrived, load_sem, send_sem, recv_sem,
 ):
     me = lax.axis_index("dev")
     loads = [
@@ -323,13 +327,14 @@
         mid[2 * t + 1] = out[:, :SLOTS]
         mid[2 * t + 2] = out[:, SLOTS:]
 
-    @pl.loop(0, 4)
+    @pl.loop(0, 2)
     def _(t):
-        forward_inner(2 * t)
-        forward_inner(2 * t + 1)
+        for n in range(4):
+            forward_inner(4 * t + n)
 
     for axis in (0, 1, 2):
         await_axis(axis, *wires[0])
+    for axis in (0, 1, 2):
         gather_far(axis, arrived.at[0], found, ghosts, nbr_src, nbr_idx, orient)
 
     high, low = split2(ghosts[0])
@@ -338,7 +343,7 @@
     mid[17] = out[:, SLOTS:]
 
     def forward_outer(t):
-        half = pl.multiple_of(32 * t, 32)
+        half = aligned(32 * t, 32)
         extra = jnp.concatenate(
             [
                 jnp.concatenate(
@@ -358,10 +363,8 @@
         mid[2 * t + 1] += out[:, :SLOTS]
         mid[2 * t + 2] += out[:, SLOTS:]
 
-    @pl.loop(0, 4)
-    def _(t):
-        forward_outer(2 * t)
-        forward_outer(2 * t + 1)
+    for t in range(8):
+        forward_outer(t)
 
     def middle(g):
         start = pl.multiple_of(16 * g, 16)
@@ -379,10 +382,10 @@
         mid[:, pl.ds(start, 8), :] = u[:, :SLOTS].reshape(NE, 8, SLOTS)
         mid[:, pl.ds(start + 8, 8), :] = u[:, SLOTS:].reshape(NE, 8, SLOTS)
 
-    @pl.loop(0, 7)
+    @pl.loop(0, 3)
     def _(g):
-        for n in range(3):
-            middle(3 * g + n)
+        for n in range(7):
+            middle(7 * g + n)
 
     def spread(first, second):
         u = jnp.concatenate([mid[first], mid[second]], axis=1)
@@ -393,14 +396,10 @@
     send_planes(0, wires[1])
     launch(0, *wires[1])
 
-    def store(t):
-        rows = pl.ds(pl.multiple_of(512 * t, 512), 512)
-        return pltpu.make_async_copy(solved.at[rows], solved_out.at[rows], store_sem.at[t])
-
     def inverse(t):
         out = dot(l5[...], spread(2 * t + 1, 2 * t + 2))
         base = pl.multiple_of(512 * t, 512)
-        half = pl.multiple_of(32 * t, 32)
+        half = aligned(32 * t, 32)
         for n in range(2):
             lanes = slice(SLOTS * n, SLOTS * n + SLOTS)
             solved[pl.ds(base + 256 * n, 256), :] = out[0:256, lanes]
@@ -412,57 +411,48 @@
                     parts[axis, 0, rows, SLOTS * side : SLOTS * side + SLOTS] = high
                     parts[axis, 1, rows, SLOTS * side : SLOTS * side + SLOTS] = low
 
-    @pl.loop(0, 4)
+    @pl.loop(0, 2)
     def _(t):
-        inverse(2 * t)
-        inverse(2 * t + 1)
+        for n in range(4):
+            inverse(4 * t + n)
 
     for axis in (2, 1):
         send_planes(axis, wires[1])
         launch(axis, *wires[1])
-    for t in range(8):
-        store(t).start()
     for axis in range(3):
         gather_near(axis, parts, found, nbr_src, nbr_idx)
     for axis in (0, 1, 2):
         await_axis(axis, *wires[1])
-        gather_far(axis, arrived.at[1], found, back_out, nbr_src, nbr_idx, orient)
-    for t in range(8):
-        store(t).wait()
-
-
-def finish_kernel(solved, back, out):
-    step = pl.program_id(0)
+    for axis in (0, 1, 2):
+        gather_far(axis, arrived.at[1], found, ghosts, nbr_src, nbr_idx, orient)
     rank = lax.broadcasted_iota(jnp.int32, (16, 16, SLOTS), 1)
-    for n in range(2):
-        half = pl.multiple_of(32 * step + 16 * n, 16)
-        base = 256 * n
-        inner = back[2, pl.ds(half, 16), :]
-        low = jnp.broadcast_to(inner[:, None, :SLOTS], (16, 16, SLOTS))
-        high = jnp.broadcast_to(inner[:, None, SLOTS:], (16, 16, SLOTS))
-        added = jnp.where(rank == 1, low, jnp.where(rank == 14, high, 0.0)).reshape(256, SLOTS)
-        out[base : base + 256, :] = solved[base : base + 256, :] + added
-        out[base + 16 : base + 32, :] += back[1, pl.ds(half, 16), :SLOTS]
-        out[base + 224 : base + 240, :] += back[1, pl.ds(half, 16), SLOTS:]
-
-    @pl.when(step == 0)
-    def _():
-        out[256:512, :] += back[0, :, :SLOTS]
-
-    @pl.when(step == 7)
-    def _():
-        out[0:256, :] += back[0, :, SLOTS:]
+
+    @pl.loop(0, 8)
+    def _(t):
+        for n in range(2):
+            half = pl.multiple_of(32 * t + 16 * n, 16)
+            base = pl.multiple_of(512 * t + 256 * n, 256)
+            inner = ghosts[2, pl.ds(half, 16), :]
+            low = jnp.broadcast_to(inner[:, None, :SLOTS], (16, 16, SLOTS))
+            high = jnp.broadcast_to(inner[:, None, SLOTS:], (16, 16, SLOTS))
+            added = jnp.where(rank == 1, low, jnp.where(rank == 14, high, 0.0)).reshape(256, SLOTS)
+            solved[pl.ds(base, 256), :] += added
+            solved[pl.ds(base + 16, 16), :] += ghosts[1, pl.ds(half, 16), :SLOTS]
+            solved[pl.ds(base + 224, 16), :] += ghosts[1, pl.ds(half, 16), SLOTS:]
+
+    solved[256:512, :] += ghosts[0, :, :SLOTS]
+    solved[14 * 256 : 15 * 256, :] += ghosts[0, :, SLOTS:]
 
 
 def shards(field, s_mats, lam, coeff, nbr_src, nbr_idx, orient, send_x, send_y, send_z):
     left, right = (jnp.asarray(table, BF) for table in make_tables())
     flat = field.reshape(4096, SLOTS)
     inputs = (flat, s_mats, lam, coeff, nbr_src, nbr_idx, orient, send_x, send_y, send_z, left, right)
-    solved, back = pl.pallas_call(
+    out = pl.pallas_call(
         smooth_kernel,
-        out_shape=(jax.ShapeDtypeStruct((4096, SLOTS), F32), jax.ShapeDtypeStruct((3, 256, 256), F32)),
-        in_specs=[pl.BlockSpec(memory_space=pl.ANY)] * 12,
-        out_specs=(pl.BlockSpec(memory_space=pl.ANY), VMEM),
+        out_shape=jax.ShapeDtypeStruct((4096, SLOTS), F32),
+        in_specs=[pl.BlockSpec(memory_space=pltpu.HBM)] * 12,
+        out_specs=VMEM,
         scratch_shapes=[pltpu.VMEM(value.shape, value.dtype) for value in inputs]
         + [
             pltpu.VMEM((ROWS, 1024), BF),
@@ -476,27 +466,15 @@
             pltpu.VMEM((3, 256, 256), F32),
             pltpu.VMEM((3, 256, 256), F32),
             pltpu.VMEM((NE, ROWS, SLOTS), F32),
-            pltpu.VMEM((4096, SLOTS), F32),
             pltpu.VMEM((192, 256), F32),
             pltpu.VMEM((2, 192, 256), F32),
             pltpu.SemaphoreType.DMA((12,)),
-            pltpu.SemaphoreType.DMA((8,)),
             pltpu.SemaphoreType.DMA((2, 6)),
             pltpu.SemaphoreType.DMA((2, 6)),
         ],
-        compiler_params=pltpu.CompilerParams(collective_id=0, has_side_effects=True),
+        compiler_params=pltpu.CompilerParams(collective_id=0, has_side_effects=True, vmem_limit_bytes=24 << 20),
         name="smooth",
-    )(*inputs)
-    whole = lambda step: (0, 0, 0)
-    some = pl.BlockSpec((512, SLOTS), lambda step: (step, 0))
-    out = pl.pallas_call(
-        finish_kernel,
-        out_shape=jax.ShapeDtypeStruct((4096, SLOTS), F32),
-        grid=(8,),
-        in_specs=[some, pl.BlockSpec((3, 256, 256), whole)],
-        out_specs=some,
-        name="finish",
-    )(solved, back)
+    )(*(pltpu.with_memory_space_constraint(value, pltpu.HBM) for value in inputs))
     return out.reshape(field.shape)
 
 

time: 32.6 us -> 24.7 us (0.76)
  Pallas kernels: 32.3 us -> 23.3 us
  local copies, waits for them, and re-layouts: 0 us -> 1.32 us
    pallas_call x2 -> x1, Pallas kernels: 32.3 us -> 23.3 us  [shards(): pl.pallas_call(smooth_kernel, out_shape=jax.ShapeDtypeStruct((4096, SLOTS...]
    unnamed x0 -> x1, local copies, waits for them, and re-layouts: none -> 1.32 us
where the time goes in v2:
time: 24.7 us; the launch traced here: 24.6 us
  Pallas kernels  23.3 us (94%)
  local copies, waits for them, and re-layouts  1.32 us (5%)
    pallas_call x1, Pallas kernels, shards(): pl.pallas_call(smooth_kernel, out_shape=jax.ShapeDtypeStruct((4096, SLOTS...  23.3 us
    unnamed x1, local copies, waits for them, and re-layouts  1.32 us

profile of v2, /device:TPU:6, one launch (start us, length us, event | category | flops | bytes accessed | tf_op | source)
XLA Modules:
  0.0 24.6 jit_solution(11275096127087036894)
XLA Ops:
  0.0 23.3 %smooth.1 = f32[4096,128]{1,0:T(8,128)S(1)} custom-call(f32[4096,128]{1,0:T(8,128)} %bitcast.3, f32[3,18,18]{2,1,0:T(8,128)} %s_mats_in.1, f32[3,18]{1,0:T(4,128)} %lam_in.1, f32[3,128]{1,0:T(4,128)} %coeff_in.1, s32[6,128]{1,0:T(8,128)} %src_in.1, s32[6,128]{1,0:T(8,128)} %idx_in.1, s32[6,128]{1,0:T(8,128)} %orient_in.1, s32[2,16]{1,0:T(2,128)} %send_x_in.1, ...), custom_call_target="tpu_custom_call" | custom-call | tf_op jit(solution)/shard_map/smooth/pallas_call | solution.py:451
  23.3 1.3 %copy.14 = f32[16,16,16,128]{3,2,1,0:T(8,128)} copy(f32[16,16,16,128]{3,2,1,0:T(8,128)S(1)} %bitcast.2) | data formatting | bytes 4194304

commit v3 on v2

--- a/solution.py
+++ b/solution.py
@@ -22,41 +22,22 @@
 
 
 def make_tables():
-    r = np.arange(ROWS)
-    fits = r < NE * NE
-    rb = np.zeros((ROWS, 96))
-    rc = np.zeros((ROWS, 96))
-    ra = np.zeros((NE * 8, 96))
-    for t in range(3):
-        rb[r[fits], t * 32 + r[fits] // NE] = 1
-        rc[r[fits], t * 32 + r[fits] % NE] = 1
-        ra[np.arange(NE * 8), t * 32 + np.arange(NE * 8) // 8] = 1
+    b, c = np.divmod(np.arange(NE * NE), NE)
+    row = np.where(c < 16, 16 * b + c, 288 + 24 * (c - 16) + b)
     inner = np.arange(1, 17)
     low, high = np.zeros(16, int), np.full(16, 17)
     jq = np.concatenate([np.repeat(inner, 16), low, high, inner, inner])
     kq = np.concatenate([np.tile(inner, 16), inner, inner, low, high])
-    rj = np.zeros((RIM, 96))
-    rk = np.zeros((RIM, 96))
-    for t in range(3):
-        rj[np.arange(RIM), t * 32 + jq] = 1
-        rk[np.arange(RIM), t * 32 + kq] = 1
     cols = np.concatenate([np.arange(256), np.tile(np.arange(256, 320), 3)])
-    qj = np.zeros((32, 512))
-    qk = np.zeros((32, 512))
+    qj, qk, qi = np.zeros((3, 32, 512))
     qj[jq[cols], np.arange(448)] = 1
     qk[kq[cols], np.arange(448)] = 1
-    qi = np.zeros((32, 512))
-    c = np.arange(432)
-    qi[(c % 144) // 8, c] = 1
-    qb = np.zeros((32, 1024))
-    qc = np.zeros((32, 1024))
-    c = np.arange(1008)
-    c = c[c % ROWS < NE * NE]
-    qb[c % ROWS // NE, c] = 1
-    qc[c % ROWS % NE, c] = 1
-    left = np.concatenate([rb, rc, ra, rj, rk])
-    right = np.concatenate([qj, qk, qi, qb[:, :512], qb[:, 512:], qc[:, :512], qc[:, 512:]])
-    return left, right
+    qi[np.arange(432) % 144 // 8, np.arange(432)] = 1
+    qb, qc = np.zeros((2, 32, 1024))
+    for t in range(3):
+        qb[b, ROWS * t + row] = 1
+        qc[c, ROWS * t + row] = 1
+    return np.concatenate([qj, qk, qi, qb, qc], axis=1)
 
 
 def split2(x):
@@ -77,10 +58,6 @@
 
 def widen(small, right):
     return sum(dot(term, right) for term in split3(small))
-
-
-def deepen(left, small):
-    return dot(left, jnp.concatenate(split3(small), axis=0))
 
 
 def pick(condition):
@@ -207,64 +184,89 @@
     return jnp.concatenate(both, axis=1)
 
 
-def product_blocks(rows, depth, left_a, left_b, small_a, small_b, columns):
-    split_a = jnp.concatenate(split3(small_a), axis=0)
-    split_b = jnp.concatenate(split3(small_b), axis=0)
-    for start in range(0, rows, depth):
-        piece = slice(start, start + depth)
-        yield piece, dot(left_a[piece, :], split_a[:, columns]) * dot(left_b[piece, :], split_b[:, columns])
-
-
-def make_operators(s_mats, lam, coeff, left, right, l1, l2, l4, l5, d12, d0):
-    rb = left.at[0:336]
-    rc = left.at[336:672]
-    ra = left.at[672:816]
-    rj = left.at[816:1136]
-    rk = left.at[1136:1456]
-    cols = lambda n: right[32 * n : 32 * n + 32, :]
+def store_terms(value, out, rows, highs, lows):
+    high, low = split2(value)
+    for start in highs:
+        out[rows, start : start + SLOTS] = high
+    for start in lows:
+        out[rows, start : start + SLOTS] = low
+
+
+def store_mixed(value, out, rows, start, bound):
+    high, low = split2(value)
+    lane = lax.broadcasted_iota(jnp.int32, value.shape, 1)
+    out[rows, start : start + SLOTS] = jnp.where(lane < bound, high.astype(F32), low.astype(F32)).astype(BF)
+
+
+def store_tile(value, out, rows, tile, bound):
+    start = SLOTS * tile
+    if start + SLOTS <= bound:
+        store_terms(value, out, rows, (start,), ())
+    elif start >= bound:
+        store_terms(value, out, rows, (), (start,))
+    else:
+        store_mixed(value, out, rows, start, bound - start)
+
+
+def make_operators(s_mats, lam, coeff, right, l1, l2, l4, l5, l5r, d12, d0):
     room = ((0, 14), (0, 14))
     mats = [jnp.pad(s_mats[axis], room) for axis in range(3)]
     turned = [jnp.pad(s_mats[axis].T, room) for axis in range(3)]
-    small = widen(turned[1], cols(0)), widen(turned[2], cols(1))
-    for piece, block in product_blocks(ROWS, 112, rb, rc, *small, slice(0, 256)):
-        high, low = split2(block)
-        l1[piece, 0:256] = high
-        l1[piece, 256:512] = high
-        l1[piece, 512:768] = low
-    lane = lax.broadcasted_iota(jnp.int32, (112, 256), 1)
-    for piece, block in product_blocks(ROWS, 112, rb, rc, *small, slice(256, 512)):
-        high, low = split2(block)
-        l1[piece, 768:1024] = jnp.where(lane < 128, high.astype(F32), low.astype(F32)).astype(BF)
-    lane = lax.broadcasted_iota(jnp.int32, (144, 256), 1)
-    row = lax.broadcasted_iota(jnp.int32, (144, 256), 0)
-    same = (lane & 7) == (row & 7)
+
+    def tail(a, b, join):
+        return jnp.concatenate([join(a[0:24], b[16:17]), join(a[0:24], b[17:18])], axis=0)
+
+    first = widen(turned[1], right[:, 0:512])
+    second = widen(turned[2], right[:, 512:1024])
+    for tile in range(4):
+        lanes = slice(SLOTS * tile, SLOTS * tile + SLOTS)
+        a, b = first[:, lanes], second[:, lanes]
+        blocks = [(slice(16 * n, 16 * n + 16), a[n : n + 1] * b[0:16]) for n in range(NE)]
+        blocks.append((slice(288, 336), tail(a, b, jnp.multiply)))
+        for rows, value in blocks:
+            if tile < 2:
+                store_terms(value, l1, rows, (SLOTS * tile, SLOTS * tile + 256), (SLOTS * tile + 512,))
+            elif tile == 2:
+                store_terms(value, l1, rows, (768,), ())
+            else:
+                store_terms(value, l1, rows, (), (896,))
+
+    same = (lax.broadcasted_iota(jnp.int32, (8, SLOTS), 0) == (lax.broadcasted_iota(jnp.int32, (8, SLOTS), 1) & 7))
     for mat, out in ((turned[0], l2), (mats[0], l4)):
-        whole = jnp.concatenate(split3(widen(mat, cols(2))), axis=0)
-        for half in range(2):
-            columns = slice(256 * half, 256 * half + 256)
-            high, low = split2(jnp.where(same, dot(ra[...], whole[:, columns]), 0.0))
-            out[:, columns] = jnp.where(lane < 288 - 256 * half, high.astype(F32), low.astype(F32)).astype(BF)
-    lane = lax.broadcasted_iota(jnp.int32, (80, 256), 1)
-    for half in range(2):
-        small = widen(mats[1], cols(3 + half)), widen(mats[2], cols(5 + half))
-        for part in range(2):
-            base = 512 * half + 256 * part
-            for piece, block in product_blocks(RIM, 80, rj, rk, *small, slice(256 * part, 256 * part + 256)):
-                high, low = split2(block)
-                l5[piece, base : base + 256] = jnp.where(
-                    lane < 2 * ROWS - base, high.astype(F32), low.astype(F32)
-                ).astype(BF)
+        wide = widen(mat, right[:, 1024:1536])
+        for tile in range(4):
+            part = wide[:, SLOTS * tile : SLOTS * tile + SLOTS]
+            for n in range(0, NE, 2):
+                value = jnp.concatenate([jnp.where(same, part[m : m + 1], 0.0) for m in (n, n + 1)], axis=0)
+                store_tile(value, out, slice(8 * n, 8 * n + 16), tile, 288)
+
+    first = widen(pltpu.roll(mats[1], 31, 0), right[:, 1536:2560])
+    second = widen(pltpu.roll(mats[2], 31, 0), right[:, 2560:3584])
+    for tile in range(8):
+        lanes = slice(SLOTS * tile, SLOTS * tile + SLOTS)
+        a, b = first[:, lanes], second[:, lanes]
+        values = [a[n : n + 1] * b[0:16] for n in (*range(16), 31, 16)]
+        values += [a[0:16] * b[n : n + 1] for n in (31, 16)]
+        for n, value in enumerate(values[:16]):
+            store_tile(value, l5, slice(16 * n, 16 * n + 16), tile, 2 * ROWS)
+        for n, value in enumerate(values[16:] if tile < 3 else ()):
+            high, low = split2(value)
+            l5r[16 * n : 16 * n + 16, lanes] = high
+            l5r[64 + 16 * n : 64 + 16 * n + 16, lanes] = low
+
     levels = jnp.pad(lam[...], ((0, 5), (0, 110))).T[:32]
     products = [levels[:, axis : axis + 1] * coeff[axis : axis + 1, :] for axis in range(3)]
-    d12[...] = deepen(rb[...], products[1]) + deepen(rc[...], products[2])
-    d0[...] = deepen(ra[...], products[0])
+    for n in range(NE):
+        d12[16 * n : 16 * n + 16, :] = products[1][n : n + 1] + products[2][0:16]
+        d0[8 * n : 8 * n + 8, :] = jnp.broadcast_to(products[0][n : n + 1], (8, SLOTS))
+    d12[288:336, :] = tail(products[1], products[2], jnp.add)
 
 
 def smooth_kernel(
-    field_in, s_mats_in, lam_in, coeff_in, src_in, idx_in, orient_in, send_x_in, send_y_in, send_z_in, left_in, right_in,
+    field_in, s_mats_in, lam_in, coeff_in, src_in, idx_in, orient_in, send_x_in, send_y_in, send_z_in, right_in,
     solved,
-    field, s_mats, lam, coeff, nbr_src, nbr_idx, orient, send_x, send_y, send_z, left, right,
-    l1, l2, l4, l5, d12, d0, send, parts, found, ghosts, mid,
+    field, s_mats, lam, coeff, nbr_src, nbr_idx, orient, send_x, send_y, send_z, right,
+    l1, l2, l4, l5, l5r, d12, d0, send, parts, found, ghosts, mid, u_high, u_low,
     msgs, arrived, load_sem, send_sem, recv_sem,
 ):
     me = lax.axis_index("dev")
@@ -272,8 +274,8 @@
         pltpu.make_async_copy(source, target, load_sem.at[n])
         for n, (source, target) in enumerate(
             (
-                (field_in, field), (send_x_in, send_x), (send_y_in, send_y), (send_z_in, send_z),
-                (left_in, left), (right_in, right), (s_mats_in, s_mats), (lam_in, lam), (coeff_in, coeff),
+                (send_x_in, send_x), (send_y_in, send_y), (send_z_in, send_z), (field_in, field),
+                (s_mats_in, s_mats), (right_in, right), (lam_in, lam), (coeff_in, coeff),
                 (src_in, nbr_src), (idx_in, nbr_idx), (orient_in, orient),
             )
         )
@@ -305,17 +307,15 @@
     def send_planes(axis, wire):
         send_axis(axis, *wire[:2], parts, send, *wire[2:])
 
-    for axis in (2, 0, 1):
+    for axis in (1, 2, 0):
         parts[axis, 0], parts[axis, 1] = split2(face_planes(axis, field))
         send_planes(axis, wires[0])
-        if axis == 2:
-            total = sum(jnp.where(flag, 1, 0) for flag in present)
-            pl.semaphore_wait(barrier, total)
+    pl.semaphore_wait(barrier, sum(jnp.where(flag, 1, 0) for flag in present))
+    for axis in (1, 2, 0):
         launch(axis, *wires[0])
-
     for load in loads[4:]:
         load.wait()
-    make_operators(s_mats, lam, coeff, left, right, l1, l2, l4, l5, d12, d0)
+    make_operators(s_mats, lam, coeff, right, l1, l2, l4, l5, l5r, d12, d0)
     for axis in range(3):
         gather_near(axis, parts, found, nbr_src, nbr_idx)
 
@@ -379,8 +379,11 @@
         z = z / (base + jnp.concatenate([d] * NE, axis=0))
         high, low = split2(z)
         u = dot(l4[:, 0:432], jnp.concatenate([high, low, high], axis=0))
-        mid[:, pl.ds(start, 8), :] = u[:, :SLOTS].reshape(NE, 8, SLOTS)
-        mid[:, pl.ds(start + 8, 8), :] = u[:, SLOTS:].reshape(NE, 8, SLOTS)
+        high, low = split2(
+            jnp.concatenate([u[:, :SLOTS].reshape(NE, 8, SLOTS), u[:, SLOTS:].reshape(NE, 8, SLOTS)], axis=1)
+        )
+        u_high[:, pl.ds(start, 16), :] = high
+        u_low[:, pl.ds(start, 16), :] = low
 
     @pl.loop(0, 3)
     def _(g):
@@ -388,37 +391,35 @@
             middle(7 * g + n)
 
     def spread(first, second):
-        u = jnp.concatenate([mid[first], mid[second]], axis=1)
-        high, low = split2(u)
-        return jnp.concatenate([high, low, high, jnp.zeros((16, 256), BF)], axis=0)
-
-    parts[0, 0], parts[0, 1] = split2(dot(l5[0:256, :], spread(0, 17)))
-    send_planes(0, wires[1])
-    launch(0, *wires[1])
-
-    def inverse(t):
-        out = dot(l5[...], spread(2 * t + 1, 2 * t + 2))
-        base = pl.multiple_of(512 * t, 512)
-        half = aligned(32 * t, 32)
-        for n in range(2):
-            lanes = slice(SLOTS * n, SLOTS * n + SLOTS)
-            solved[pl.ds(base + 256 * n, 256), :] = out[0:256, lanes]
-            for axis in (1, 2):
-                for side in (0, 1):
-                    start = 256 + 32 * (axis - 1) + 16 * side
-                    high, low = split2(out[start : start + 16, lanes])
-                    rows = pl.ds(half + 16 * n, 16)
-                    parts[axis, 0, rows, SLOTS * side : SLOTS * side + SLOTS] = high
-                    parts[axis, 1, rows, SLOTS * side : SLOTS * side + SLOTS] = low
-
-    @pl.loop(0, 2)
-    def _(t):
-        for n in range(4):
-            inverse(4 * t + n)
-
-    for axis in (2, 1):
+        high = jnp.concatenate([u_high[first], u_high[second]], axis=1)
+        low = jnp.concatenate([u_low[first], u_low[second]], axis=1)
+        return high, low
+
+    def inverse(first, second):
+        high, low = spread(first, second)
+        return dot(l5[...], jnp.concatenate([high, low, high, jnp.zeros((16, 256), BF)], axis=0))
+
+    for t in range(8):
+        high, low = spread(2 * t + 1, 2 * t + 2)
+        both = dot(l5r[:, 0:ROWS], high)
+        out = both[0:64] + both[64:128] + dot(l5r[0:64, 0:ROWS], low)
+        for axis in (1, 2):
+            for side in (0, 1):
+                start = 32 * (axis - 1) + 16 * side
+                rows = slice(32 * t, 32 * t + 32)
+                lanes = slice(SLOTS * side, SLOTS * side + SLOTS)
+                block = out[start : start + 16]
+                block = jnp.concatenate([block[:, :SLOTS], block[:, SLOTS:]], axis=0)
+                parts[axis, 0, rows, lanes], parts[axis, 1, rows, lanes] = split2(block)
+    parts[0, 0], parts[0, 1] = split2(inverse(0, 17))
+    for axis in (1, 2, 0):
         send_planes(axis, wires[1])
+    for axis in (1, 2, 0):
         launch(axis, *wires[1])
+    for t in range(8):
+        out = inverse(2 * t + 1, 2 * t + 2)
+        solved[512 * t : 512 * t + 256, :] = out[:, :SLOTS]
+        solved[512 * t + 256 : 512 * t + 512, :] = out[:, SLOTS:]
     for axis in range(3):
         gather_near(axis, parts, found, nbr_src, nbr_idx)
     for axis in (0, 1, 2):
@@ -445,20 +446,21 @@
 
 
 def shards(field, s_mats, lam, coeff, nbr_src, nbr_idx, orient, send_x, send_y, send_z):
-    left, right = (jnp.asarray(table, BF) for table in make_tables())
+    right = jnp.asarray(make_tables(), BF)
     flat = field.reshape(4096, SLOTS)
-    inputs = (flat, s_mats, lam, coeff, nbr_src, nbr_idx, orient, send_x, send_y, send_z, left, right)
+    inputs = (flat, s_mats, lam, coeff, nbr_src, nbr_idx, orient, send_x, send_y, send_z, right)
     out = pl.pallas_call(
         smooth_kernel,
         out_shape=jax.ShapeDtypeStruct((4096, SLOTS), F32),
-        in_specs=[pl.BlockSpec(memory_space=pltpu.HBM)] * 12,
+        in_specs=[pl.BlockSpec(memory_space=pltpu.HBM)] * 11,
         out_specs=VMEM,
         scratch_shapes=[pltpu.VMEM(value.shape, value.dtype) for value in inputs]
         + [
             pltpu.VMEM((ROWS, 1024), BF),
             pltpu.VMEM((144, 512), BF),
             pltpu.VMEM((144, 512), BF),
-            pltpu.VMEM((RIM, 1024), BF),
+            pltpu.VMEM((256, 1024), BF),
+            pltpu.VMEM((128, 384), BF),
             pltpu.VMEM((ROWS, SLOTS), F32),
             pltpu.VMEM((144, SLOTS), F32),
             pltpu.VMEM((8, SLOTS), jnp.int32),
@@ -466,9 +468,11 @@
             pltpu.VMEM((3, 256, 256), F32),
             pltpu.VMEM((3, 256, 256), F32),
             pltpu.VMEM((NE, ROWS, SLOTS), F32),
+            pltpu.VMEM((NE, ROWS, SLOTS), BF),
+            pltpu.VMEM((NE, ROWS, SLOTS), BF),
             pltpu.VMEM((192, 256), F32),
             pltpu.VMEM((2, 192, 256), F32),
-            pltpu.SemaphoreType.DMA((12,)),
+            pltpu.SemaphoreType.DMA((11,)),
             pltpu.SemaphoreType.DMA((2, 6)),
             pltpu.SemaphoreType.DMA((2, 6)),
         ],

time: 24.7 us -> 22.7 us (0.919)
  Pallas kernels: 23.3 us -> 21.3 us
    pallas_call x1, Pallas kernels: 23.3 us -> 21.3 us  [shards(): pl.pallas_call(smooth_kernel, out_shape=jax.ShapeDtypeStruct((4096, SLOTS...]
where the time goes in v3:
time: 22.7 us; the launch traced here: 22.6 us
  Pallas kernels  21.3 us (94%)
  local copies, waits for them, and re-layouts  1.32 us (6%)
    pallas_call x1, Pallas kernels, shards(): pl.pallas_call(smooth_kernel, out_shape=jax.ShapeDtypeStruct((4096, SLOTS...  21.3 us
    unnamed x1, local copies, waits for them, and re-layouts  1.32 us

profile of v3, /device:TPU:6, one launch (start us, length us, event | category | flops | bytes accessed | tf_op | source)
XLA Modules:
  0.0 22.6 jit_solution(11785717161882103945)
XLA Ops:
  0.0 21.3 %smooth.1 = f32[4096,128]{1,0:T(8,128)S(1)} custom-call(f32[4096,128]{1,0:T(8,128)} %bitcast.3, f32[3,18,18]{2,1,0:T(8,128)} %s_mats_in.1, f32[3,18]{1,0:T(4,128)} %lam_in.1, f32[3,128]{1,0:T(4,128)} %coeff_in.1, s32[6,128]{1,0:T(8,128)} %src_in.1, s32[6,128]{1,0:T(8,128)} %idx_in.1, s32[6,128]{1,0:T(8,128)} %orient_in.1, s32[2,16]{1,0:T(2,128)} %send_x_in.1, ...), custom_call_target="tpu_custom_call" | custom-call | tf_op jit(solution)/shard_map/smooth/pallas_call | solution.py:452
  21.3 1.3 %copy.13 = f32[16,16,16,128]{3,2,1,0:T(8,128)} copy(f32[16,16,16,128]{3,2,1,0:T(8,128)S(1)} %bitcast.2) | data formatting | bytes 4194304

commit v4 on v3

--- a/solution.py
+++ b/solution.py
@@ -30,14 +30,16 @@
     kq = np.concatenate([np.tile(inner, 16), inner, inner, low, high])
     cols = np.concatenate([np.arange(256), np.tile(np.arange(256, 320), 3)])
     qj, qk, qi = np.zeros((3, 32, 512))
+    qe = np.zeros((32, SLOTS))
     qj[jq[cols], np.arange(448)] = 1
     qk[kq[cols], np.arange(448)] = 1
     qi[np.arange(432) % 144 // 8, np.arange(432)] = 1
+    qe[1 + np.arange(128) // 8, np.arange(128)] = 1
     qb, qc = np.zeros((2, 32, 1024))
     for t in range(3):
         qb[b, ROWS * t + row] = 1
         qc[c, ROWS * t + row] = 1
-    return np.concatenate([qj, qk, qi, qb, qc], axis=1)
+    return np.concatenate([qj, qk, qi, qb, qc, qe], axis=1)
 
 
 def split2(x):
@@ -66,6 +68,10 @@
 
 def aligned(index, step):
     return index if isinstance(index, int) else pl.multiple_of(index, step)
+
+
+def face_index(face):
+    return (slice(None),) * (face // 2) + (14 if face % 2 else 1,)
 
 
 def list_rows(direction):
@@ -171,19 +177,6 @@
                 out[axis, 16 * u + 8 * n : 16 * u + 8 * n + 8, lanes] = jnp.where(second[:, lanes], turned, rows[n])
 
 
-def face_planes(axis, field):
-    if axis == 0:
-        both = [field[256:512, :], field[14 * 256 : 15 * 256, :]]
-    elif axis == 1:
-        both = [
-            jnp.concatenate([field[256 * i + 16 * j : 256 * i + 16 * j + 16, :] for i in range(16)], axis=0)
-            for j in (1, 14)
-        ]
-    else:
-        both = [field[pl.ds(k, 256, stride=16), :] for k in (1, 14)]
-    return jnp.concatenate(both, axis=1)
-
-
 def store_terms(value, out, rows, highs, lows):
     high, low = split2(value)
     for start in highs:
@@ -208,7 +201,7 @@
         store_mixed(value, out, rows, start, bound - start)
 
 
-def make_operators(s_mats, lam, coeff, right, l1, l2, l4, l5, l5r, d12, d0):
+def make_operators(s_mats, lam, coeff, right, l1, l2, l4, l5, l5r, d12, d0, factors):
     room = ((0, 14), (0, 14))
     mats = [jnp.pad(s_mats[axis], room) for axis in range(3)]
     turned = [jnp.pad(s_mats[axis].T, room) for axis in range(3)]
@@ -232,13 +225,17 @@
                 store_terms(value, l1, rows, (), (896,))
 
     same = (lax.broadcasted_iota(jnp.int32, (8, SLOTS), 0) == (lax.broadcasted_iota(jnp.int32, (8, SLOTS), 1) & 7))
-    for mat, out in ((turned[0], l2), (mats[0], l4)):
-        wide = widen(mat, right[:, 1024:1536])
-        for tile in range(4):
-            part = wide[:, SLOTS * tile : SLOTS * tile + SLOTS]
-            for n in range(0, NE, 2):
-                value = jnp.concatenate([jnp.where(same, part[m : m + 1], 0.0) for m in (n, n + 1)], axis=0)
-                store_tile(value, out, slice(8 * n, 8 * n + 16), tile, 288)
+    wide = widen(turned[0], right[:, 3584:3712])
+    for n in range(0, NE, 2):
+        rows = slice(8 * n, 8 * n + 16)
+        value = jnp.concatenate([jnp.where(same, wide[m : m + 1, :SLOTS], 0.0) for m in (n, n + 1)], axis=0)
+        store_terms(value, l2, rows, (0, 128), (256,))
+    wide = widen(mats[0], right[:, 1024:1536])
+    for tile in range(4):
+        part = wide[:, SLOTS * tile : SLOTS * tile + SLOTS]
+        for n in range(0, NE, 2):
+            value = jnp.concatenate([jnp.where(same, part[m : m + 1], 0.0) for m in (n, n + 1)], axis=0)
+            store_tile(value, l4, slice(8 * n, 8 * n + 16), tile, 288)
 
     first = widen(pltpu.roll(mats[1], 31, 0), right[:, 1536:2560])
     second = widen(pltpu.roll(mats[2], 31, 0), right[:, 2560:3584])
@@ -259,6 +256,10 @@
     for n in range(NE):
         d12[16 * n : 16 * n + 16, :] = products[1][n : n + 1] + products[2][0:16]
         d0[8 * n : 8 * n + 8, :] = jnp.broadcast_to(products[0][n : n + 1], (8, SLOTS))
+    sides = [jnp.broadcast_to(turned[0][:, n : n + 1], (32, SLOTS)) for n in (0, 17)]
+    for n in range(NE):
+        for m in (0, 1):
+            factors[m, 8 * n : 8 * n + 8, :] = jnp.broadcast_to(sides[m][n : n + 1], (8, SLOTS))
     d12[288:336, :] = tail(products[1], products[2], jnp.add)
 
 
@@ -266,7 +267,7 @@
     field_in, s_mats_in, lam_in, coeff_in, src_in, idx_in, orient_in, send_x_in, send_y_in, send_z_in, right_in,
     solved,
     field, s_mats, lam, coeff, nbr_src, nbr_idx, orient, send_x, send_y, send_z, right,
-    l1, l2, l4, l5, l5r, d12, d0, send, parts, found, ghosts, mid, u_high, u_low,
+    planes, l1, l2, l4, l5, l5r, d12, d0, factors, send, parts, found, ghosts, mid, coef, edges, shells, u_high, u_low,
     msgs, arrived, load_sem, send_sem, recv_sem,
 ):
     me = lax.axis_index("dev")
@@ -274,7 +275,8 @@
         pltpu.make_async_copy(source, target, load_sem.at[n])
         for n, (source, target) in enumerate(
             (
-                (send_x_in, send_x), (send_y_in, send_y), (send_z_in, send_z), (field_in, field),
+                (send_x_in, send_x), (send_y_in, send_y), (send_z_in, send_z),
+                *((field_in.at[face_index(face)], planes.at[face]) for face in (2, 3, 4, 5, 0, 1)), (field_in, field),
                 (s_mats_in, s_mats), (right_in, right), (lam_in, lam), (coeff_in, coeff),
                 (src_in, nbr_src), (idx_in, nbr_idx), (orient_in, orient),
             )
@@ -292,7 +294,7 @@
                 arrived[phase, start : start + count, :] = jnp.zeros((count, 256), F32)
 
     barrier = greet(me, present)
-    for load in loads[:4]:
+    for load in loads[:9]:
         load.wait()
     send[...] = jnp.full((8, SLOTS), -1, jnp.int32)
     send[0:1, 0:16] = send_x[0:1, :]
@@ -307,21 +309,22 @@
     def send_planes(axis, wire):
         send_axis(axis, *wire[:2], parts, send, *wire[2:])
 
-    for axis in (1, 2, 0):
-        parts[axis, 0], parts[axis, 1] = split2(face_planes(axis, field))
+    for axis in (2, 1, 0):
+        parts[axis, 0], parts[axis, 1] = split2(
+            jnp.concatenate([planes[2 * axis + n].reshape(256, SLOTS) for n in (0, 1)], axis=1)
+        )
         send_planes(axis, wires[0])
     pl.semaphore_wait(barrier, sum(jnp.where(flag, 1, 0) for flag in present))
-    for axis in (1, 2, 0):
+    for axis in (2, 1, 0):
         launch(axis, *wires[0])
-    for load in loads[4:]:
+    for load in loads[9:]:
         load.wait()
-    make_operators(s_mats, lam, coeff, right, l1, l2, l4, l5, l5r, d12, d0)
+    make_operators(s_mats, lam, coeff, right, l1, l2, l4, l5, l5r, d12, d0, factors)
     for axis in range(3):
         gather_near(axis, parts, found, nbr_src, nbr_idx)
 
     def forward_inner(t):
-        base = pl.multiple_of(512 * t, 512)
-        x = jnp.concatenate([field[pl.ds(base, 256), :], field[pl.ds(base + 256, 256), :]], axis=1)
+        x = jnp.concatenate([field[2 * t + n].reshape(256, SLOTS) for n in (0, 1)], axis=1)
         high, low = split2(x)
         out = dot(l1[:, 0:768], jnp.concatenate([high, low, high], axis=0))
         mid[2 * t + 1] = out[:, :SLOTS]
@@ -332,51 +335,84 @@
         for n in range(4):
             forward_inner(4 * t + n)
 
+    @pl.loop(0, 3)
+    def _(g):
+        for n in range(7):
+            start = pl.multiple_of(112 * g + 16 * n, 16)
+            block = mid[1:17, pl.ds(start, 16), :]
+            y = jnp.concatenate([block[:, 0:8].reshape(SLOTS, SLOTS), block[:, 8:16].reshape(SLOTS, SLOTS)], axis=1)
+            high, low = split2(y)
+            z = dot(l2[:, 0:384], jnp.concatenate([high, low, high], axis=0))
+            coef[:, pl.ds(start, 8), :] = z[:, :SLOTS].reshape(NE, 8, SLOTS)
+            coef[:, pl.ds(start + 8, 8), :] = z[:, SLOTS:].reshape(NE, 8, SLOTS)
+
     for axis in (0, 1, 2):
         await_axis(axis, *wires[0])
     for axis in (0, 1, 2):
         gather_far(axis, arrived.at[0], found, ghosts, nbr_src, nbr_idx, orient)
 
+    turned = []
+    for axis in (1, 2):
+        for half in range(2):
+            x = ghosts[axis].reshape(16, 16, 256)[:, 8 * half : 8 * half + 8, :].reshape(SLOTS, 256)
+            high, low = split2(x)
+            turned.append(dot(l2[:, 0:384], jnp.concatenate([high, low, high], axis=0)))
     high, low = split2(ghosts[0])
     out = dot(l1[:, 0:768], jnp.concatenate([high, low, high], axis=0))
-    mid[0] = out[:, :SLOTS]
-    mid[17] = out[:, SLOTS:]
-
-    def forward_outer(t):
-        half = aligned(32 * t, 32)
+    edges[0] = out[:, :SLOTS]
+    edges[1] = out[:, SLOTS:]
+    for a in range(0, NE, 2):
         extra = jnp.concatenate(
             [
                 jnp.concatenate(
                     [
-                        ghosts[axis, pl.ds(half + 16 * n, 16), SLOTS * side : SLOTS * side + SLOTS]
-                        for axis in (1, 2)
+                        turned[2 * axis + half][8 * n : 8 * n + 8, SLOTS * side : SLOTS * side + SLOTS]
+                        for axis in (0, 1)
                         for side in (0, 1)
+                        for half in (0, 1)
                     ],
                     axis=0,
                 )
-                for n in (0, 1)
+                for n in (a, a + 1)
             ],
             axis=1,
         )
         high, low = split2(extra)
         out = dot(l1[:, 768:960], jnp.concatenate([high, low, high], axis=0))
-        mid[2 * t + 1] += out[:, :SLOTS]
-        mid[2 * t + 2] += out[:, SLOTS:]
-
-    for t in range(8):
-        forward_outer(t)
-
+        coef[a] += out[:, :SLOTS]
+        coef[a + 1] += out[:, SLOTS:]
+    for a in range(0, NE, 2):
+        scaled = []
+        for n in (a, a + 1):
+            rows = slice(8 * n, 8 * n + 8)
+            z = coef[n].reshape(42, 8, SLOTS)
+            for m in (0, 1):
+                z = z + factors[m, rows, :] * edges[m].reshape(42, 8, SLOTS)
+            z = (z / (d0[rows, :] + d12[...].reshape(42, 8, SLOTS))).reshape(ROWS, SLOTS)
+            coef[n] = z
+            scaled.append(z)
+        high, low = split2(jnp.concatenate(scaled, axis=1))
+        both = dot(l5r[:, 0:ROWS], high)
+        out = both[0:64] + both[64:128] + dot(l5r[0:64, 0:ROWS], low)
+        shells[a] = out[:, :SLOTS]
+        shells[a + 1] = out[:, SLOTS:]
+    for axis in (2, 1):
+        turned = []
+        for half in range(2):
+            starts = [32 * (axis - 1) + 16 * side + 8 * half for side in (0, 1)]
+            x = jnp.concatenate([shells[:, start : start + 8, :].reshape(144, SLOTS) for start in starts], axis=1)
+            high, low = split2(x)
+            turned.append(dot(l4[:, 0:432], jnp.concatenate([high, low, high], axis=0)))
+        rim = jnp.concatenate([turned[half][8 * i : 8 * i + 8] for i in range(1, 17) for half in range(2)], axis=0)
+        parts[axis, 0], parts[axis, 1] = split2(rim)
+    for axis in (2, 1):
+        send_planes(axis, wires[1])
+    for axis in (2, 1):
+        launch(axis, *wires[1])
     def middle(g):
         start = pl.multiple_of(16 * g, 16)
-        block = mid[:, pl.ds(start, 16), :]
-        y = jnp.concatenate([block[:, 0:8].reshape(144, SLOTS), block[:, 8:16].reshape(144, SLOTS)], axis=1)
-        high, low = split2(y)
-        z = dot(l2[:, 0:432], jnp.concatenate([high, low, high], axis=0))
-        d = d12[pl.ds(start, 16), :]
-        d = jnp.concatenate([d[0:8], d[8:16]], axis=1)
-        base = d0[...]
-        base = jnp.concatenate([base, base], axis=1)
-        z = z / (base + jnp.concatenate([d] * NE, axis=0))
+        block = coef[:, pl.ds(start, 16), :]
+        z = jnp.concatenate([block[:, 0:8].reshape(144, SLOTS), block[:, 8:16].reshape(144, SLOTS)], axis=1)
         high, low = split2(z)
         u = dot(l4[:, 0:432], jnp.concatenate([high, low, high], axis=0))
         high, low = split2(
@@ -390,32 +426,14 @@
         for n in range(7):
             middle(7 * g + n)
 
-    def spread(first, second):
+    def inverse(first, second):
         high = jnp.concatenate([u_high[first], u_high[second]], axis=1)
         low = jnp.concatenate([u_low[first], u_low[second]], axis=1)
-        return high, low
-
-    def inverse(first, second):
-        high, low = spread(first, second)
         return dot(l5[...], jnp.concatenate([high, low, high, jnp.zeros((16, 256), BF)], axis=0))
 
-    for t in range(8):
-        high, low = spread(2 * t + 1, 2 * t + 2)
-        both = dot(l5r[:, 0:ROWS], high)
-        out = both[0:64] + both[64:128] + dot(l5r[0:64, 0:ROWS], low)
-        for axis in (1, 2):
-            for side in (0, 1):
-                start = 32 * (axis - 1) + 16 * side
-                rows = slice(32 * t, 32 * t + 32)
-                lanes = slice(SLOTS * side, SLOTS * side + SLOTS)
-                block = out[start : start + 16]
-                block = jnp.concatenate([block[:, :SLOTS], block[:, SLOTS:]], axis=0)
-                parts[axis, 0, rows, lanes], parts[axis, 1, rows, lanes] = split2(block)
     parts[0, 0], parts[0, 1] = split2(inverse(0, 17))
-    for axis in (1, 2, 0):
-        send_planes(axis, wires[1])
-    for axis in (1, 2, 0):
-        launch(axis, *wires[1])
+    send_planes(0, wires[1])
+    launch(0, *wires[1])
     for t in range(8):
         out = inverse(2 * t + 1, 2 * t + 2)
         solved[512 * t : 512 * t + 256, :] = out[:, :SLOTS]
@@ -447,8 +465,7 @@
 
 def shards(field, s_mats, lam, coeff, nbr_src, nbr_idx, orient, send_x, send_y, send_z):
     right = jnp.asarray(make_tables(), BF)
-    flat = field.reshape(4096, SLOTS)
-    inputs = (flat, s_mats, lam, coeff, nbr_src, nbr_idx, orient, send_x, send_y, send_z, right)
+    inputs = (field, s_mats, lam, coeff, nbr_src, nbr_idx, orient, send_x, send_y, send_z, right)
     out = pl.pallas_call(
         smooth_kernel,
         out_shape=jax.ShapeDtypeStruct((4096, SLOTS), F32),
@@ -456,23 +473,28 @@
         out_specs=VMEM,
         scratch_shapes=[pltpu.VMEM(value.shape, value.dtype) for value in inputs]
         + [
+            pltpu.VMEM((6, 16, 16, SLOTS), F32),
             pltpu.VMEM((ROWS, 1024), BF),
-            pltpu.VMEM((144, 512), BF),
+            pltpu.VMEM((144, 384), BF),
             pltpu.VMEM((144, 512), BF),
             pltpu.VMEM((256, 1024), BF),
             pltpu.VMEM((128, 384), BF),
             pltpu.VMEM((ROWS, SLOTS), F32),
             pltpu.VMEM((144, SLOTS), F32),
+            pltpu.VMEM((2, 144, SLOTS), F32),
             pltpu.VMEM((8, SLOTS), jnp.int32),
             pltpu.VMEM((3, 2, 256, 256), BF),
             pltpu.VMEM((3, 256, 256), F32),
             pltpu.VMEM((3, 256, 256), F32),
             pltpu.VMEM((NE, ROWS, SLOTS), F32),
+            pltpu.VMEM((NE, ROWS, SLOTS), F32),
+            pltpu.VMEM((2, ROWS, SLOTS), F32),
+            pltpu.VMEM((NE, 64, SLOTS), F32),
             pltpu.VMEM((NE, ROWS, SLOTS), BF),
             pltpu.VMEM((NE, ROWS, SLOTS), BF),
             pltpu.VMEM((192, 256), F32),
             pltpu.VMEM((2, 192, 256), F32),
-            pltpu.SemaphoreType.DMA((11,)),
+            pltpu.SemaphoreType.DMA((17,)),
             pltpu.SemaphoreType.DMA((2, 6)),
             pltpu.SemaphoreType.DMA((2, 6)),
         ],

time: 22.7 us -> 21 us (0.925)
  Pallas kernels: 21.3 us -> 19.5 us
    pallas_call x1, Pallas kernels: 21.3 us -> 19.5 us  [shards(): pl.pallas_call(smooth_kernel, out_shape=jax.ShapeDtypeStruct((4096, SLOTS...]
where the time goes in v4:
time: 21 us; the launch traced here: 20.8 us
  Pallas kernels  19.5 us (93%)
  local copies, waits for them, and re-layouts  1.32 us (6%)
    pallas_call x1, Pallas kernels, shards(): pl.pallas_call(smooth_kernel, out_shape=jax.ShapeDtypeStruct((4096, SLOTS...  19.5 us
    unnamed x1, local copies, waits for them, and re-layouts  1.32 us

profile of v4, /device:TPU:6, one launch (start us, length us, event | category | flops | bytes accessed | tf_op | source)
XLA Modules:
  0.0 20.8 jit_solution(11085866574425160405)
XLA Ops:
  0.0 19.5 %smooth.1 = f32[4096,128]{1,0:T(8,128)S(1)} custom-call(f32[16,16,16,128]{3,2,1,0:T(8,128)} %field_in.1, f32[3,18,18]{2,1,0:T(8,128)} %s_mats_in.1, f32[3,18]{1,0:T(4,128)} %lam_in.1, f32[3,128]{1,0:T(4,128)} %coeff_in.1, s32[6,128]{1,0:T(8,128)} %src_in.1, s32[6,128]{1,0:T(8,128)} %idx_in.1, s32[6,128]{1,0:T(8,128)} %orient_in.1, s32[2,16]{1,0:T(2,128)} %send_x_in.1, ...), custom_call_target="tpu_custom_call" | custom-call | tf_op jit(solution)/shard_map/smooth/pallas_call | solution.py:469
  19.5 1.3 %copy.13 = f32[16,16,16,128]{3,2,1,0:T(8,128)} copy(f32[16,16,16,128]{3,2,1,0:T(8,128)S(1)} %bitcast.1) | data formatting | bytes 4194304

commit v5 on v4

--- a/solution.py
+++ b/solution.py
@@ -265,12 +265,22 @@
 
 def smooth_kernel(
     field_in, s_mats_in, lam_in, coeff_in, src_in, idx_in, orient_in, send_x_in, send_y_in, send_z_in, right_in,
-    solved,
+    solved, back,
     field, s_mats, lam, coeff, nbr_src, nbr_idx, orient, send_x, send_y, send_z, right,
     planes, l1, l2, l4, l5, l5r, d12, d0, factors, send, parts, found, ghosts, mid, coef, edges, shells, u_high, u_low,
     msgs, arrived, load_sem, send_sem, recv_sem,
 ):
     me = lax.axis_index("dev")
+    present = find_neighbours(me)
+    for direction in range(6):
+        start, count = list_rows(direction)
+
+        @pl.when(jnp.logical_not(present[direction ^ 1]))
+        def _():
+            for phase in range(2):
+                arrived[phase, start : start + count, :] = jnp.zeros((count, 256), F32)
+
+    barrier = greet(me, present)
     loads = [
         pltpu.make_async_copy(source, target, load_sem.at[n])
         for n, (source, target) in enumerate(
@@ -284,16 +294,6 @@
     ]
     for load in loads:
         load.start()
-    present = find_neighbours(me)
-    for direction in range(6):
-        start, count = list_rows(direction)
-
-        @pl.when(jnp.logical_not(present[direction ^ 1]))
-        def _():
-            for phase in range(2):
-                arrived[phase, start : start + count, :] = jnp.zeros((count, 256), F32)
-
-    barrier = greet(me, present)
     for load in loads[:9]:
         load.wait()
     send[...] = jnp.full((8, SLOTS), -1, jnp.int32)
@@ -330,21 +330,16 @@
         mid[2 * t + 1] = out[:, :SLOTS]
         mid[2 * t + 2] = out[:, SLOTS:]
 
-    @pl.loop(0, 2)
-    def _(t):
-        for n in range(4):
-            forward_inner(4 * t + n)
-
-    @pl.loop(0, 3)
-    def _(g):
-        for n in range(7):
-            start = pl.multiple_of(112 * g + 16 * n, 16)
-            block = mid[1:17, pl.ds(start, 16), :]
-            y = jnp.concatenate([block[:, 0:8].reshape(SLOTS, SLOTS), block[:, 8:16].reshape(SLOTS, SLOTS)], axis=1)
-            high, low = split2(y)
-            z = dot(l2[:, 0:384], jnp.concatenate([high, low, high], axis=0))
-            coef[:, pl.ds(start, 8), :] = z[:, :SLOTS].reshape(NE, 8, SLOTS)
-            coef[:, pl.ds(start + 8, 8), :] = z[:, SLOTS:].reshape(NE, 8, SLOTS)
+    for t in range(8):
+        forward_inner(t)
+
+    for start in range(0, ROWS, 16):
+        block = mid[1:17, start : start + 16, :]
+        y = jnp.concatenate([block[:, 0:8].reshape(SLOTS, SLOTS), block[:, 8:16].reshape(SLOTS, SLOTS)], axis=1)
+        high, low = split2(y)
+        z = dot(l2[:, 0:384], jnp.concatenate([high, low, high], axis=0))
+        coef[:, start : start + 8, :] = z[:, :SLOTS].reshape(NE, 8, SLOTS)
+        coef[:, start + 8 : start + 16, :] = z[:, SLOTS:].reshape(NE, 8, SLOTS)
 
     for axis in (0, 1, 2):
         await_axis(axis, *wires[0])
@@ -443,34 +438,46 @@
     for axis in (0, 1, 2):
         await_axis(axis, *wires[1])
     for axis in (0, 1, 2):
-        gather_far(axis, arrived.at[1], found, ghosts, nbr_src, nbr_idx, orient)
+        gather_far(axis, arrived.at[1], found, back, nbr_src, nbr_idx, orient)
+
+
+def finish_kernel(solved, back, out, whole, sems):
     rank = lax.broadcasted_iota(jnp.int32, (16, 16, SLOTS), 1)
 
-    @pl.loop(0, 8)
-    def _(t):
-        for n in range(2):
-            half = pl.multiple_of(32 * t + 16 * n, 16)
-            base = pl.multiple_of(512 * t + 256 * n, 256)
-            inner = ghosts[2, pl.ds(half, 16), :]
-            low = jnp.broadcast_to(inner[:, None, :SLOTS], (16, 16, SLOTS))
-            high = jnp.broadcast_to(inner[:, None, SLOTS:], (16, 16, SLOTS))
-            added = jnp.where(rank == 1, low, jnp.where(rank == 14, high, 0.0)).reshape(256, SLOTS)
-            solved[pl.ds(base, 256), :] += added
-            solved[pl.ds(base + 16, 16), :] += ghosts[1, pl.ds(half, 16), :SLOTS]
-            solved[pl.ds(base + 224, 16), :] += ghosts[1, pl.ds(half, 16), SLOTS:]
-
-    solved[256:512, :] += ghosts[0, :, :SLOTS]
-    solved[14 * 256 : 15 * 256, :] += ghosts[0, :, SLOTS:]
+    def store(t):
+        rows = pl.ds(512 * t, 512)
+        return pltpu.make_async_copy(whole.at[rows], out.at[rows], sems.at[t])
+
+    for i in range(16):
+        base = 256 * i
+        half = slice(16 * i, 16 * i + 16)
+        inner = back[2, half, :]
+        low = jnp.broadcast_to(inner[:, None, :SLOTS], (16, 16, SLOTS))
+        high = jnp.broadcast_to(inner[:, None, SLOTS:], (16, 16, SLOTS))
+        value = solved[base : base + 256, :]
+        value = value + jnp.where(rank == 1, low, jnp.where(rank == 14, high, 0.0)).reshape(256, SLOTS)
+        if i in (1, 14):
+            lanes = slice(0, SLOTS) if i == 1 else slice(SLOTS, 2 * SLOTS)
+            value = value + back[0, :, lanes]
+        whole[base : base + 16, :] = value[0:16]
+        whole[base + 16 : base + 32, :] = value[16:32] + back[1, half, :SLOTS]
+        whole[base + 32 : base + 224, :] = value[32:224]
+        whole[base + 224 : base + 240, :] = value[224:240] + back[1, half, SLOTS:]
+        whole[base + 240 : base + 256, :] = value[240:256]
+        if i % 2 == 1:
+            store(i // 2).start()
+    for t in range(8):
+        store(t).wait()
 
 
 def shards(field, s_mats, lam, coeff, nbr_src, nbr_idx, orient, send_x, send_y, send_z):
     right = jnp.asarray(make_tables(), BF)
     inputs = (field, s_mats, lam, coeff, nbr_src, nbr_idx, orient, send_x, send_y, send_z, right)
-    out = pl.pallas_call(
+    solved, back = pl.pallas_call(
         smooth_kernel,
-        out_shape=jax.ShapeDtypeStruct((4096, SLOTS), F32),
+        out_shape=(jax.ShapeDtypeStruct((4096, SLOTS), F32), jax.ShapeDtypeStruct((3, 256, 256), F32)),
         in_specs=[pl.BlockSpec(memory_space=pltpu.HBM)] * 11,
-        out_specs=VMEM,
+        out_specs=(VMEM, VMEM),
         scratch_shapes=[pltpu.VMEM(value.shape, value.dtype) for value in inputs]
         + [
             pltpu.VMEM((6, 16, 16, SLOTS), F32),
@@ -501,6 +508,15 @@
         compiler_params=pltpu.CompilerParams(collective_id=0, has_side_effects=True, vmem_limit_bytes=24 << 20),
         name="smooth",
     )(*(pltpu.with_memory_space_constraint(value, pltpu.HBM) for value in inputs))
+    out = pl.pallas_call(
+        finish_kernel,
+        out_shape=jax.ShapeDtypeStruct((4096, SLOTS), F32),
+        in_specs=[VMEM, VMEM],
+        out_specs=pl.BlockSpec(memory_space=pltpu.HBM),
+        scratch_shapes=[pltpu.VMEM((4096, SLOTS), F32), pltpu.SemaphoreType.DMA((8,))],
+        compiler_params=pltpu.CompilerParams(vmem_limit_bytes=8 << 20),
+        name="finish",
+    )(solved, back)
     return out.reshape(field.shape)
 
 

time: 21 us -> 20.7 us (0.986)
  local copies, waits for them, and re-layouts: 1.32 us -> 0 us
  Pallas kernels: 19.5 us -> 20.4 us
    unnamed x1 -> x0, local copies, waits for them, and re-layouts: 1.32 us -> none
    pallas_call x1 -> x2, Pallas kernels: 19.5 us -> 20.4 us  [the longest x1 19 us: shards(): pl.pallas_call(smooth_kernel, out_shape=(jax.ShapeDtypeStruct((4096, SLOT...]
where the time goes in v5:
time: 20.7 us; the launch traced here: 20.4 us
  Pallas kernels  20.4 us (99%)
    pallas_call x1, Pallas kernels, shards(): pl.pallas_call(smooth_kernel, out_shape=(jax.ShapeDtypeStruct((4096, SLOT...  19 us
    pallas_call x1, Pallas kernels, shards(): pl.pallas_call(finish_kernel, out_shape=jax.ShapeDtypeStruct((4096, SLOTS...  1.43 us

profile of v5, /device:TPU:6, one launch (start us, length us, event | category | flops | bytes accessed | tf_op | source)
XLA Modules:
  0.0 20.4 jit_solution(11155344547171366810)
XLA Ops:
  0.0 19.0 %smooth.1 = (f32[4096,128]{1,0:T(8,128)S(1)}, f32[3,256,256]{2,1,0:T(8,128)S(1)}) custom-call(f32[16,16,16,128]{3,2,1,0:T(8,128)} %field_in.1, f32[3,18,18]{2,1,0:T(8,128)} %s_mats_in.1, f32[3,18]{1,0:T(4,128)} %lam_in.1, f32[3,128]{1,0:T(4,128)} %coeff_in.1, s32[6,128]{1,0:T(8,128)} %src_in.1, s32[6,128]{1,0:T(8,128)} %idx_in.1, s32[6,128]{1,0:T(8,128)} %orient_in.1, ...), custom_call_target="tpu_custom_call" | custom-call | tf_op jit(solution)/shard_map/smooth/pallas_call | solution.py:476
  19.0 1.4 %finish.1 = f32[4096,128]{1,0:T(8,128)} custom-call(f32[4096,128]{1,0:T(8,128)S(1)} %get-tuple-element.7.solved, f32[3,256,256]{2,1,0:T(8,128)S(1)} %get-tuple-element.8.back), custom_call_target="tpu_custom_call" | custom-call | tf_op jit(solution)/shard_map/finish/pallas_call | solution.py:511

commit v6 on v5

--- a/solution.py
+++ b/solution.py
@@ -285,20 +285,22 @@
         pltpu.make_async_copy(source, target, load_sem.at[n])
         for n, (source, target) in enumerate(
             (
-                (send_x_in, send_x), (send_y_in, send_y), (send_z_in, send_z),
-                *((field_in.at[face_index(face)], planes.at[face]) for face in (2, 3, 4, 5, 0, 1)), (field_in, field),
+                (send_z_in, send_z), (send_y_in, send_y),
+                *((field_in.at[face_index(face)], planes.at[face]) for face in (4, 5, 2, 3)),
+                (send_x_in, send_x),
+                *((field_in.at[face_index(face)], planes.at[face]) for face in (0, 1)),
                 (s_mats_in, s_mats), (right_in, right), (lam_in, lam), (coeff_in, coeff),
-                (src_in, nbr_src), (idx_in, nbr_idx), (orient_in, orient),
+                (field_in, field), (src_in, nbr_src), (idx_in, nbr_idx), (orient_in, orient),
             )
         )
     ]
-    for load in loads:
+    for load in loads[:9]:
         load.start()
-    for load in loads[:9]:
+    for load in loads[:6]:
         load.wait()
+    for load in loads[9:]:
+        load.start()
     send[...] = jnp.full((8, SLOTS), -1, jnp.int32)
-    send[0:1, 0:16] = send_x[0:1, :]
-    send[0:1, 16:32] = send_x[1:2, :]
     send[1:2, 0:16] = send_y[0:1, :]
     send[1:2, 16:32] = send_y[1:2, :]
     send[2:3, 0:64] = send_z[0:1, :]
@@ -309,14 +311,23 @@
     def send_planes(axis, wire):
         send_axis(axis, *wire[:2], parts, send, *wire[2:])
 
-    for axis in (2, 1, 0):
+    def prepare(axis):
         parts[axis, 0], parts[axis, 1] = split2(
             jnp.concatenate([planes[2 * axis + n].reshape(256, SLOTS) for n in (0, 1)], axis=1)
         )
         send_planes(axis, wires[0])
+
+    for axis in (2, 1):
+        prepare(axis)
     pl.semaphore_wait(barrier, sum(jnp.where(flag, 1, 0) for flag in present))
-    for axis in (2, 1, 0):
+    for axis in (2, 1):
         launch(axis, *wires[0])
+    for load in loads[6:9]:
+        load.wait()
+    send[0:1, 0:16] = send_x[0:1, :]
+    send[0:1, 16:32] = send_x[1:2, :]
+    prepare(0)
+    launch(0, *wires[0])
     for load in loads[9:]:
         load.wait()
     make_operators(s_mats, lam, coeff, right, l1, l2, l4, l5, l5r, d12, d0, factors)

time: 20.7 us -> 20.6 us (level)
  no operation moved by 1% of the time
where the time goes in v6:
time: 20.6 us; the launch traced here: 20.4 us
  Pallas kernels  20.4 us (99%)
    pallas_call x1, Pallas kernels, shards(): pl.pallas_call(smooth_kernel, out_shape=(jax.ShapeDtypeStruct((4096, SLOT...  19 us
    pallas_call x1, Pallas kernels, shards(): pl.pallas_call(finish_kernel, out_shape=jax.ShapeDtypeStruct((4096, SLOTS...  1.43 us

profile of v6, /device:TPU:6, one launch (start us, length us, event | category | flops | bytes accessed | tf_op | source)
XLA Modules:
  0.0 20.4 jit_solution(6618985590182335253)
XLA Ops:
  0.0 19.0 %smooth.1 = (f32[4096,128]{1,0:T(8,128)S(1)}, f32[3,256,256]{2,1,0:T(8,128)S(1)}) custom-call(f32[16,16,16,128]{3,2,1,0:T(8,128)} %field_in.1, f32[3,18,18]{2,1,0:T(8,128)} %s_mats_in.1, f32[3,18]{1,0:T(4,128)} %lam_in.1, f32[3,128]{1,0:T(4,128)} %coeff_in.1, s32[6,128]{1,0:T(8,128)} %src_in.1, s32[6,128]{1,0:T(8,128)} %idx_in.1, s32[6,128]{1,0:T(8,128)} %orient_in.1, ...), custom_call_target="tpu_custom_call" | custom-call | tf_op jit(solution)/shard_map/smooth/pallas_call | solution.py:487
  19.0 1.4 %finish.1 = f32[4096,128]{1,0:T(8,128)} custom-call(f32[4096,128]{1,0:T(8,128)S(1)} %get-tuple-element.7.solved, f32[3,256,256]{2,1,0:T(8,128)S(1)} %get-tuple-element.8.back), custom_call_target="tpu_custom_call" | custom-call | tf_op jit(solution)/shard_map/finish/pallas_call | solution.py:522
